TPU v7x, 256 devices: a whole 4x4x8 slice. The times are simulated.
256 devices in a mesh: sx: 16 (over y, x), sy: 8 (over z), freq: 2 (over core).
Axes of the slice: x: 4, y: 4, z: 8, core: 2. Of those that a mesh axis runs over, the one named last changes fastest.
Arguments:
- update_basis: bfloat16 [4, 4096, 32, 1024], P('freq', ('sx', 'sy')), may hold values from -0.1875 to 0.1875
- update_coeff: bfloat16 [4, 4096, 32, 128], P('freq', ('sx', 'sy')), may hold values from -6 to 6
- owner: int32 [4096, 1], P(('sx', 'sy')), may hold values from 0 to 15; in each aligned block of 32 rows (0 to 31, 32 to 63, ...) at most 4 rows name the same one
- sep_rhs: bfloat16 [4, 16, 8, 1024, 128], P('freq', 'sx', 'sy'), may hold values from -6 to 6
- coupling: float32 [4, 16, 8, 4, 1024], P('freq', 'sx', 'sy'), may hold values from 0.1 to 0.25
- frontal_inverse: bfloat16 [4, 16, 8, 1024, 1024], P('freq', 'sx', 'sy'), may hold values from -0.2 to 1.2
Outputs:
- solution: float32 [4, 16, 8, 1024, 128], P('freq', 'sx', 'sy')
- residual_total: float32 [], replicated
Inputs may be any that keep to these rules, and one draw needn't show every extreme that they name: In the 32 children of one grid position no owner appears more than 4 times; in every draw some owner appears exactly 4 times at some position.
All inputs are finite; a program needn't handle non-finite values.
Results may differ from a plain program's by a relative error of at most 0.0019.
Values may be sent and summed in bfloat16 or wider, within the bound.
No kernel may reach another device: no remote copies, remote signals or barrier semaphores. Data moves between devices by JAX's collectives and lax.ppermute only.
A program may use at most 128 MiB of HBM per device.

v0:
```python
import jax
import jax.numpy as jnp
from jax import lax
from jax.experimental import pallas as pl
from jax.experimental.pallas import tpu as pltpu
from jax.sharding import Mesh
from jax.sharding import PartitionSpec as P


SWEEPS = 2
SIDE = 4
CAP = 4
TILE = 256
SX = ("sx_0", "sx_1")
SX_SY = ("sx_0", "sx_1", "sy")
LOW, HIGH = (0, 1), (3, 2)


def cost(flops, bytes_accessed):
    return pl.CostEstimate(flops=flops, bytes_accessed=bytes_accessed, transcendentals=0)


def room(mebibytes):
    return pltpu.CompilerParams(vmem_limit_bytes=mebibytes << 20)


def fill_slots(owner_ref, slots, used):
    children = owner_ref.shape[0]
    for o in range(SIDE * SIDE):
        used[o] = 0
    for s in range(SIDE * SIDE * CAP):
        slots[s] = children

    def put(c, carry):
        o = owner_ref[c]
        k = used[o]
        slots[o * CAP + k] = c
        used[o] = k + 1
        return carry

    lax.fori_loop(0, children, put, 0)


def owner_at(table_ref, f, ahead, beside):
    offsets = (ahead, beside) if f == 0 else (beside, ahead)
    row = lax.rem(table_ref[0] + offsets[0], SIDE)
    column = lax.rem(table_ref[1] + offsets[1], SIDE)
    return row * SIDE + column


def multiply(weights, stacked, out, at):
    rhs_count = out.shape[1]
    turned = weights[...].T
    for s in range(0, stacked.shape[1], TILE):
        product = jnp.dot(turned, stacked[:, s : s + TILE], preferred_element_type=jnp.float32)
        for b in range(2):
            piece = product[b * rhs_count : (b + 1) * rhs_count]
            out[at + b, :, s : s + TILE] = piece.astype(out.dtype)


def put_weights(weights, coeff_ref, f, c, filled, b, k):
    rank, rhs_count = coeff_ref.shape[2:]
    at = (b * CAP + k) * rank
    coeff = coeff_ref[f, c]
    weights[at : at + rank, b * rhs_count : (b + 1) * rhs_count] = jnp.where(
        filled, coeff, jnp.zeros_like(coeff)
    )


def owner_products(plan, shapes, owners, place, basis, coeff, after=(), fetched=False):
    _, children, rank, sep_size = basis.shape
    rhs_count = coeff.shape[3]
    count = len(plan) if fetched else 1
    depth = 2 * CAP * rank

    def body(owner_ref, table_ref, basis_ref, coeff_ref, *rest):
        outs = rest[len(after) : len(after) + len(shapes)]
        slots, used, stacked, weights = rest[len(after) + len(shapes) :][:4]
        arrived = rest[-1]
        fill_slots(owner_ref, slots, used)

        def child(f, ahead, beside, k):
            c = slots[owner_at(table_ref, f, ahead, beside) * CAP + k]
            filled = c < children
            return jnp.where(filled, c, 0), filled

        def copies(n):
            _, _, f, ahead, pair = plan[n]
            return [
                pltpu.make_async_copy(
                    basis_ref.at[f, child(f, ahead, beside, k)[0]],
                    stacked.at[n, pl.ds((b * CAP + k) * rank, rank)],
                    arrived.at[n],
                )
                for b, beside in enumerate(pair)
                for k in range(CAP)
            ]

        if fetched:
            flights = [copies(n) for n in range(len(plan))]
            for flight in flights:
                for copy in flight:
                    copy.start()
        weights[...] = jnp.zeros_like(weights)
        for n, (out, at, f, ahead, pair) in enumerate(plan):
            for b, beside in enumerate(pair):
                for k in range(CAP):
                    c, filled = child(f, ahead, beside, k)
                    put_weights(weights, coeff_ref, f, c, filled, b, k)
                    if not fetched:
                        stacked[0, pl.ds((b * CAP + k) * rank, rank)] = basis_ref[f, c]
            if fetched:
                for copy in flights[n]:
                    copy.wait()
            multiply(weights, stacked.at[n if fetched else 0], outs[out], at)

    space = pltpu.MemorySpace.HBM if fetched else pltpu.MemorySpace.VMEM
    return pl.pallas_call(
        body,
        in_specs=[pl.BlockSpec(memory_space=pltpu.MemorySpace.SMEM)] * 2
        + [pl.BlockSpec(memory_space=space), pl.BlockSpec(memory_space=pltpu.MemorySpace.VMEM)]
        + [pl.BlockSpec(memory_space=pl.ANY) for _ in after],
        out_specs=[pl.BlockSpec(memory_space=pltpu.MemorySpace.VMEM) for _ in shapes],
        scratch_shapes=[
            pltpu.SMEM((SIDE * SIDE * CAP,), jnp.int32),
            pltpu.SMEM((SIDE * SIDE,), jnp.int32),
            pltpu.VMEM((count, depth, sep_size), jnp.bfloat16),
            pltpu.VMEM((depth, 2 * rhs_count), jnp.bfloat16),
            pltpu.SemaphoreType.DMA((count,)),
        ],
        out_shape=[jax.ShapeDtypeStruct((n, rhs_count, sep_size), dtype) for n, dtype in shapes],
        compiler_params=room(53 if fetched else 16),
        cost_estimate=cost(
            2 * len(plan) * 4 * CAP * rank * sep_size * rhs_count * 2,
            len(plan) * 2 * (CAP * rank * sep_size * 2 + rhs_count * sep_size * 4),
        ),
    )(owners, place, basis, coeff, *after)


def in_vmem(count):
    return [pl.BlockSpec(memory_space=pltpu.MemorySpace.VMEM)] * count


def join(mine, got, whole):
    def body(mine_ref, got_ref, whole_ref, out_ref):
        n = mine_ref.shape[0]
        out_ref[:n] = (mine_ref[...] + got_ref[...].astype(jnp.float32)).astype(out_ref.dtype)

    return pl.pallas_call(
        body,
        in_specs=in_vmem(3),
        out_specs=in_vmem(1)[0],
        out_shape=jax.ShapeDtypeStruct(whole.shape, whole.dtype),
        input_output_aliases={2: 0},
        compiler_params=room(4),
        cost_estimate=cost(mine.size * 2, mine.size * 8),
    )(mine, got, whole)


def row_totals(own, low, high):
    _, rhs_count, sep_size = own.shape

    def body(own_ref, low_ref, high_ref, *outs):
        for at, out in enumerate(outs):
            crossed = (at + 2) % SIDE
            total = own_ref[at] + low_ref[at].astype(jnp.float32) + high_ref[crossed].astype(jnp.float32)
            out[...] = total.astype(out.dtype)

    types = (jnp.float32,) * 3 + (jnp.bfloat16,)
    return pl.pallas_call(
        body,
        in_specs=in_vmem(3),
        out_specs=in_vmem(SIDE),
        out_shape=[jax.ShapeDtypeStruct((rhs_count, sep_size), dtype) for dtype in types],
        compiler_params=room(4),
        cost_estimate=cost(own.size * 2, own.size * 12),
    )(own, low, high)


def across(field, matrix_tile):
    return lax.dot_general(
        field, matrix_tile, (((1,), (1,)), ((), ())), preferred_element_type=jnp.float32
    )


def staged(sep_rhs, matrix):
    f_local, sep_size, rhs_count = sep_rhs.shape

    def body(rhs_ref, matrix_ref, out_ref, held_ref):
        for f in range(f_local):
            for s in range(0, sep_size, TILE):
                out_ref[f, :, s : s + TILE] = rhs_ref[f, s : s + TILE, :].astype(jnp.float32).T
                held_ref[f, s : s + TILE] = matrix_ref[f, s : s + TILE]

    return pl.pallas_call(
        body,
        in_specs=in_vmem(2),
        out_specs=in_vmem(2),
        out_shape=[
            jax.ShapeDtypeStruct((f_local, rhs_count, sep_size), jnp.float32),
            jax.ShapeDtypeStruct(matrix.shape, matrix.dtype),
        ],
        compiler_params=room(4),
        cost_estimate=cost(sep_rhs.size, sep_rhs.size * 6 + matrix.size * 4),
    )(sep_rhs, matrix)


def solve_cost(rhs_count, sep_size):
    return cost(2 * sep_size * sep_size * rhs_count, sep_size * (2 * sep_size + 24 * rhs_count))


def first_solve(f, rhs, parts, matrix):
    _, rhs_count, sep_size = rhs.shape

    def body(rhs_ref, *rest):
        parts_refs, (matrix_ref, right_ref, out_ref, sent_ref) = rest[:-4], rest[-4:]
        right = rhs_ref[f]
        for part in parts_refs:
            right = right - part[...].astype(jnp.float32)
        right_ref[...] = right
        field = right.astype(jnp.bfloat16)
        for s in range(0, sep_size, TILE):
            out = across(field, matrix_ref[f, s : s + TILE])
            out_ref[:, s : s + TILE] = out
            sent_ref[:, s : s + TILE] = out.astype(jnp.bfloat16)

    types = (jnp.float32, jnp.float32, jnp.bfloat16)
    return pl.pallas_call(
        body,
        in_specs=in_vmem(2 + len(parts)),
        out_specs=in_vmem(3),
        out_shape=[jax.ShapeDtypeStruct((rhs_count, sep_size), t) for t in types],
        compiler_params=room(6),
        cost_estimate=solve_cost(rhs_count, sep_size),
    )(rhs, *parts, matrix)


def residual_of(f, table_ref, right_ref, mine_ref, around_refs, coupling_ref):
    residual = right_ref[...] - mine_ref[...]
    for n, around in enumerate(around_refs):
        coupled = coupling_ref[f, pl.ds(table_ref[2 + n], 1), :]
        coupled = jnp.where(table_ref[6 + n] > 0, coupled, jnp.zeros_like(coupled))
        residual = residual + coupled * around[...].astype(jnp.float32)
    return residual


def sweep(f, table, right_side, mine, around, coupling, matrix):
    rhs_count, sep_size = mine.shape

    def body(table_ref, right_ref, mine_ref, *rest):
        around_refs, (coupling_ref, matrix_ref, out_ref, sent_ref) = rest[:4], rest[4:]
        residual = residual_of(f, table_ref, right_ref, mine_ref, around_refs, coupling_ref)
        field = residual.astype(jnp.bfloat16)
        for s in range(0, sep_size, TILE):
            out = mine_ref[:, s : s + TILE] + across(field, matrix_ref[f, s : s + TILE])
            out_ref[:, s : s + TILE] = out
            sent_ref[:, s : s + TILE] = out.astype(jnp.bfloat16)

    return pl.pallas_call(
        body,
        in_specs=[pl.BlockSpec(memory_space=pltpu.MemorySpace.SMEM)] + in_vmem(8),
        out_specs=in_vmem(2),
        out_shape=[jax.ShapeDtypeStruct(mine.shape, t) for t in (jnp.float32, jnp.bfloat16)],
        compiler_params=room(6),
        cost_estimate=solve_cost(rhs_count, sep_size),
    )(table, right_side, mine, *around, coupling, matrix)


def last_sweep(f, table, right_side, mine, around, coupling, matrix, before, copies):
    rhs_count, sep_size = mine.shape
    f_local = matrix.shape[0]

    def body(table_ref, right_ref, mine_ref, *rest):
        around_refs, (coupling_ref, matrix_ref), rest = rest[:4], rest[4:6], rest[6:]
        out_ref, sum_ref = rest[len(before) :]
        residual = residual_of(f, table_ref, right_ref, mine_ref, around_refs, coupling_ref)
        field = residual.astype(jnp.bfloat16)
        square = jnp.sum(residual * residual, axis=0, keepdims=True)
        total = jnp.sum(square * table_ref[10 + f].astype(jnp.float32))
        total = jnp.broadcast_to(total, sum_ref.shape)
        sum_ref[...] = total + rest[1][...] if before else total
        for s in range(0, sep_size, TILE):
            step = across(matrix_ref[f, s : s + TILE], field)
            out_ref[0, s : s + TILE, :] = mine_ref[:, s : s + TILE].T + step

    return pl.pallas_call(
        body,
        grid=(1,),
        in_specs=[pl.BlockSpec(memory_space=pltpu.MemorySpace.SMEM)]
        + in_vmem(8)
        + ([pl.BlockSpec(memory_space=pl.ANY)] + in_vmem(1) if before else []),
        out_specs=[pl.BlockSpec((1, sep_size, rhs_count), lambda i: (f, 0, 0)), in_vmem(1)[0]],
        out_shape=[
            jax.ShapeDtypeStruct((f_local, sep_size, rhs_count), jnp.float32),
            jax.ShapeDtypeStruct((copies, 8, 128), jnp.float32),
        ],
        input_output_aliases={9: 0} if before else {},
        compiler_params=room(6),
        cost_estimate=solve_cost(rhs_count, sep_size),
    )(table, right_side, mine, *around, coupling, matrix, *before)


def turn(x, axis, by):
    return lax.ppermute(x, axis, [(i, (i + by) % SIDE) for i in range(SIDE)])


def neighbours(x, axis, count):
    pairs = [[(i, (i + 1) % count) for i in range(first, count, 2)] for first in range(2)]
    return tuple(lax.ppermute(x, axis, p + [(b, a) for a, b in p]) for p in pairs)


def on_device(update_basis, update_coeff, owner, sep_rhs, coupling, frontal_inverse):
    f_local = update_basis.shape[0]
    sep_size = update_basis.shape[3]
    rhs_count = update_coeff.shape[3]
    columns, rows = lax.axis_size(SX), lax.axis_size("sy")
    odd = [lax.rem(lax.axis_index(axis).astype(jnp.int32), 2) for axis in (SX, "sy")]
    freq_ids = [lax.axis_index("freq").astype(jnp.int32) * f_local + f + 1 for f in range(f_local)]
    place = [lax.axis_index(axis).astype(jnp.int32) for axis in SX]
    rows_of = [1 - odd[0], odd[0], 3 - odd[1], 2 + odd[1]]
    inside = []
    for axis, count in ((SX, columns), ("sy", rows)):
        at = lax.axis_index(axis)
        inside += [jnp.int32(1), ((at > 0) & (at < count - 1)).astype(jnp.int32)]
    table = jnp.stack(place + rows_of + inside + [i * i for i in freq_ids])
    data = (owner[:, 0], table, update_basis, update_coeff)
    half, full = jnp.bfloat16, jnp.float32

    axes = (SX, SX[::-1])
    plan = tuple((2 * f + n, 0, f, 2, pair) for f in range(2) for n, pair in enumerate((LOW, HIGH)))
    far = owner_products(plan, ((2, half),) * 4, *data, fetched=True)
    got = [(turn(far[2 * f], axes[f][0], 1), turn(far[2 * f + 1], axes[f][0], -1)) for f in range(2)]

    sides = ((1, LOW, HIGH), (3, HIGH, LOW))
    plan = tuple(
        (4 * late + 2 * f + n, 2 * late, f, ahead, pairs[late])
        for f in range(2)
        for n, (ahead, *pairs) in enumerate(sides)
        for late in range(2)
    )
    near = owner_products(plan, ((2, full),) * 4 + ((4, half),) * 4, *data)

    sums, joined = [], []
    for f in range(2):
        following = join(near[2 * f], got[f][0], near[4 + 2 * f])
        preceding = join(near[2 * f + 1], got[f][1], near[5 + 2 * f])
        joined += [following, preceding]
        sums.append((turn(following, axes[f][0], 1), turn(preceding, axes[f][0], -1)))
    plan = tuple((f, 2 * n, f, 0, pair) for f in range(2) for n, pair in enumerate((LOW, HIGH)))
    own = owner_products(plan, ((4, full),) * 2, *data, after=tuple(joined))
    rhs, matrix = staged(sep_rhs[:, 0, 0], frontal_inverse[:, 0, 0])

    coupling_rows = coupling[:, 0, 0]
    order = (1, 0)
    right_side, mine, sent = {}, {}, {}
    for f in order:
        here, following, preceding, opposite = row_totals(own[f], *sums[f])
        axis = axes[f][1]
        opposite = turn(opposite, axis, 2)
        parts = (opposite, turn(following, axis, 1), turn(preceding, axis, -1))
        right_side[f], mine[f], sent[f] = first_solve(f, rhs, (here, *parts), matrix)
    for _ in range(SWEEPS - 1):
        for f in order:
            around = neighbours(sent[f], SX, columns) + neighbours(sent[f], "sy", rows)
            mine[f], sent[f] = sweep(f, table, right_side[f], mine[f], around, coupling_rows, matrix)
    group = ("sy", "freq")
    done = ()
    for f in order:
        around = neighbours(sent[f], SX, columns) + neighbours(sent[f], "sy", rows)
        done = last_sweep(
            f, table, right_side[f], mine[f], around, coupling_rows, matrix, done, lax.axis_size(group)
        )
    solution, squares = done
    squares = jnp.sum(lax.all_to_all(squares, group, 0, 0, tiled=True), axis=0)
    squares = jnp.broadcast_to(squares, (columns, *squares.shape))
    squares = jnp.sum(lax.all_to_all(squares, SX, 0, 0, tiled=True), axis=0)
    entries = float(f_local * lax.axis_size("freq") * columns * rows * sep_size * rhs_count)
    residual_total = jnp.sqrt(squares[0, 0] / entries + 1e-06)
    return (solution[:, None, None], residual_total)


def solution(mesh):
    finer = Mesh(
        mesh.devices.reshape(SIDE, SIDE, mesh.shape["sy"], mesh.shape["freq"]),
        ("sx_0", "sx_1", "sy", "freq"),
    )

    return jax.shard_map(
        on_device,
        mesh=finer,
        in_specs=(
            P("freq", SX_SY, None, None),
            P("freq", SX_SY, None, None),
            P(SX_SY, None),
            P("freq", SX, "sy", None, None),
            P("freq", SX, "sy", None, None),
            P("freq", SX, "sy", None, None),
        ),
        out_specs=(P("freq", SX, "sy", None, None), P()),
        check_vma=False,
    )
```

profile of v0, /device:TPU:1, one launch (start us, length us, event | category | flops | bytes accessed | tf_op | source)
XLA Modules:
  0.0 144.7 jit_solution(16678491358546826918)
XLA Ops:
  0.8 0.8 copy-done.5
  1.6 5.5 %shard_map.79 = (bf16[2,128,1024]{2,1,0:T(8,128)(2,1)S(1)}, bf16[2,128,1024]{2,1,0:T(8,128)(2,1)}, bf16[2,128,1024]{2,1,0:T(8,128)(2,1)}, bf16[2,128,1024]{2,1,0:T(8,128)(2,1)}) custom-call(s32[32]{0:T(128)S(1)} %bitcast.24, s32[12]{0:T(128)S(1)} %stack.51.table_ref, bf16[2,32,32,1024]{3,2,1,0:T(8,128)(2,1)} %basis_ref.5, bf16[2,32,32,128]{3,2,1,0:T(8,128)(2,1)} %coeff_ref.5), custom_call_target="tpu_custom_call" | custom-call | flops 1073741824 | bytes 6291456 | tf_op jit(solution)/shard_map/pallas_call | solution.py:118
  7.1 3.3 %collective-permute-start.3 = (bf16[2,128,1024]{2,1,0:T(8,128)(2,1)}, bf16[2,128,1024]{2,1,0:T(8,128)(2,1)S(1)}, u32[]{:S(2)}, u32[]{:S(2)}) collective-permute-start(bf16[2,128,1024]{2,1,0:T(8,128)(2,1)} %get-tuple-element.51), channel_id=1, source_target_pairs={{0,48},{16,0},{32,16},{48,32},{1,49},{17,1},{33,17},{49,33},{2,50}... | collective-permute-start | bytes 1572872 | tf_op jit(solution)/shard_map/ppermute | solution.py:304
  10.4 2.9 %collective-permute-start.1 = (bf16[2,128,1024]{2,1,0:T(8,128)(2,1)}, bf16[2,128,1024]{2,1,0:T(8,128)(2,1)S(1)}, u32[]{:S(2)}, u32[]{:S(2)}) collective-permute-start(bf16[2,128,1024]{2,1,0:T(8,128)(2,1)} %get-tuple-element.45), channel_id=1, source_target_pairs={{0,192},{64,0},{128,64},{192,128},{1,193},{65,1},{129,65},{193,129... | collective-permute-start | bytes 1572872 | tf_op jit(solution)/shard_map/ppermute | solution.py:304
  13.3 2.4 %shard_map.78 = (f32[2,128,1024]{2,1,0:T(8,128)S(1)}, f32[2,128,1024]{2,1,0:T(8,128)S(1)}, f32[2,128,1024]{2,1,0:T(8,128)S(1)}, f32[2,128,1024]{2,1,0:T(8,128)S(...) custom-call(s32[32]{0:T(128)S(1)} %bitcast.25, ...), custom_call_target="tpu_custom_call" | custom-call | flops 2147483648 | bytes 12582912 | tf_op jit(solution)/shard_map/pallas_call | solution.py:118
  15.7 5.6 %collective-permute-done.3.got_ref = bf16[2,128,1024]{2,1,0:T(8,128)(2,1)S(1)} collective-permute-done((bf16[2,128,1024]{2,1,0:T(8,128)(2,1)}, bf16[2,128,1024]{2,1,0:T(8,128)(2,1)S(1)}, u32[]{:S(2)}, u32[]{:S(2)}) %collective-permute-start.3) | collective-permute-done | bytes 524320 | tf_op jit(solution)/shard_map/ppermute | solution.py:304
  21.5 3.4 %collective-permute-start.18 = (bf16[4,128,1024]{2,1,0:T(8,128)(2,1)S(1)}, bf16[4,128,1024]{2,1,0:T(8,128)(2,1)S(1)}, u32[]{:S(2)}, u32[]{:S(2)}) collective-permute-start(bf16[4,128,1024]{2,1,0:T(8,128)(2,1)S(1)} %shard_map.83.rest_3_), channel_id=1, source_target_pairs={{0,48},{16,0},{32,16},{48,32},{1,49},{17,1},{33,17},{49,33},{2,50}... | collective-permute-start | bytes 3145736 | tf_op jit(solution)/shard_map/ppermute | solution.py:304
  25.1 2.9 %collective-permute-start.5 = (bf16[4,128,1024]{2,1,0:T(8,128)(2,1)S(1)}, bf16[4,128,1024]{2,1,0:T(8,128)(2,1)S(1)}, u32[]{:S(2)}, u32[]{:S(2)}) collective-permute-start(bf16[4,128,1024]{2,1,0:T(8,128)(2,1)S(1)} %shard_map.81.rest_1_), channel_id=1, source_target_pairs={{0,192},{64,0},{128,64},{192,128},{1,193},{65,1},{129,65},{193,129... | collective-permute-start | bytes 3145736 | tf_op jit(solution)/shard_map/ppermute | solution.py:304
  28.3 1.8 %shard_map.84 = (f32[4,128,1024]{2,1,0:T(8,128)S(1)}, f32[4,128,1024]{2,1,0:T(8,128)S(1)}) custom-call(s32[32]{0:T(128)S(1)} %bitcast.26, s32[12]{0:T(128)S(1)} %stack.51.table_ref, bf16[2,32,32,1024]{3,2,1,0:T(8,128)(2,1)S(1)} %copy-done, bf16[2,32,32,128]{3,2,1,0:T(8,128)(2,1)S(1)} %copy-done.2, bf16[4,128,1024]{2,1,0:T(8,128)(2,1)S(1)} %shard_map.80.rest_0_, ...), custom_call_target="tpu_custom_call" | custom-call | flops 1073741824 | bytes 6291456 | tf_op jit(solution)/shard_map/pallas_call | solution.py:118
  30.1 15.7 %collective-permute-done.18.high_ref = bf16[4,128,1024]{2,1,0:T(8,128)(2,1)S(1)} collective-permute-done((bf16[4,128,1024]{2,1,0:T(8,128)(2,1)S(1)}, bf16[4,128,1024]{2,1,0:T(8,128)(2,1)S(1)}, u32[]{:S(2)}, u32[]{:S(2)}) %collective-permute-start.18) | collective-permute-done | bytes 1048608 | tf_op jit(solution)/shard_map/ppermute | solution.py:304
  45.8 3.3 %collective-permute-done.17.low_ref = bf16[4,128,1024]{2,1,0:T(8,128)(2,1)S(1)} collective-permute-done((bf16[4,128,1024]{2,1,0:T(8,128)(2,1)S(1)}, bf16[4,128,1024]{2,1,0:T(8,128)(2,1)S(1)}, u32[]{:S(2)}, u32[]{:S(2)}) %collective-permute-start.17) | collective-permute-done | bytes 1048608 | tf_op jit(solution)/shard_map/ppermute | solution.py:304
  49.1 0.3 shard_map.88
  49.4 1.4 collective-permute-start.20
  50.9 1.6 %collective-permute-start.21 = (f32[128,1024]{1,0:T(8,128)S(1)}, f32[128,1024]{1,0:T(8,128)S(1)}, u32[]{:S(2)}, u32[]{:S(2)}) collective-permute-start(f32[128,1024]{1,0:T(8,128)S(1)} %get-tuple-element.68), channel_id=1, source_target_pairs={{0,192},{64,0},{128,64},{192,128},{1,193},{65,1},{129,65},{193,129... | collective-permute-start | bytes 1572872 | tf_op jit(solution)/shard_map/ppermute | solution.py:304
  52.5 1.3 collective-permute-start.19
  53.8 0.3 shard_map.85
  54.2 2.7 %collective-permute-start.8 = (f32[128,1024]{1,0:T(8,128)S(1)}, f32[128,1024]{1,0:T(8,128)S(1)}, u32[]{:S(2)}, u32[]{:S(2)}) collective-permute-start(f32[128,1024]{1,0:T(8,128)S(1)} %get-tuple-element.57), channel_id=1, source_target_pairs={{0,48},{16,0},{32,16},{48,32},{1,49},{17,1},{33,17},{49,33},{2,50}... | collective-permute-start | bytes 1572872 | tf_op jit(solution)/shard_map/ppermute | solution.py:304
  56.8 11.4 %collective-permute-done.19.rest_1_ = bf16[128,1024]{1,0:T(8,128)(2,1)S(1)} collective-permute-done((bf16[128,1024]{1,0:T(8,128)(2,1)S(1)}, bf16[128,1024]{1,0:T(8,128)(2,1)S(1)}, u32[]{:S(2)}, u32[]{:S(2)}) %collective-permute-start.19) | collective-permute-done | bytes 262176 | tf_op jit(solution)/shard_map/ppermute | solution.py:304
  68.2 1.5 %collective-permute-start.6 = (bf16[128,1024]{1,0:T(8,128)(2,1)S(1)}, bf16[128,1024]{1,0:T(8,128)(2,1)S(1)}, u32[]{:S(2)}, u32[]{:S(2)}) collective-permute-start(bf16[128,1024]{1,0:T(8,128)(2,1)S(1)} %get-tuple-element.55), channel_id=1, source_target_pairs={{0,32},{16,48},{32,0},{48,16},{1,33},{17,49},{33,1},{49,17},{2,34}... | collective-permute-start | bytes 786440 | tf_op jit(solution)/shard_map/ppermute | solution.py:304
  69.8 0.4 shard_map.77
  70.2 0.9 shard_map.89
  71.1 2.1 %collective-permute-start.22 = (bf16[128,1024]{1,0:T(8,128)(2,1)S(1)}, bf16[128,1024]{1,0:T(8,128)(2,1)S(1)}, u32[]{:S(2)}, u32[]{:S(2)}) collective-permute-start(bf16[128,1024]{1,0:T(8,128)(2,1)S(1)} %get-tuple-element.71), channel_id=1, source_target_pairs={{0,16},{32,48},{64,80},{96,112},{128,144},{160,176},{192,208},{224... | collective-permute-start | bytes 786440 | tf_op jit(solution)/shard_map/ppermute | solution.py:309
  73.2 0.3 collective-permute-start.23
  73.5 1.4 %collective-permute-done.6.rest_1_ = bf16[128,1024]{1,0:T(8,128)(2,1)S(1)} collective-permute-done((bf16[128,1024]{1,0:T(8,128)(2,1)S(1)}, bf16[128,1024]{1,0:T(8,128)(2,1)S(1)}, u32[]{:S(2)}, u32[]{:S(2)}) %collective-permute-start.6) | collective-permute-done | bytes 262176 | tf_op jit(solution)/shard_map/ppermute | solution.py:304
  75.0 1.6 %collective-permute-start.24 = (bf16[128,1024]{1,0:T(8,128)(2,1)S(1)}, bf16[128,1024]{1,0:T(8,128)(2,1)S(1)}, u32[]{:S(2)}, u32[]{:S(2)}) collective-permute-start(bf16[128,1024]{1,0:T(8,128)(2,1)S(1)} %get-tuple-element.71), channel_id=1, source_target_pairs={{0,2},{4,6},{8,10},{12,14},{2,0},{6,4},{10,8},{14,12},{1,3},{5,7},... | collective-permute-start | bytes 786440 | tf_op jit(solution)/shard_map/ppermute | solution.py:309
  76.6 4.7 %collective-permute-start.25 = (bf16[128,1024]{1,0:T(8,128)(2,1)S(1)}, bf16[128,1024]{1,0:T(8,128)(2,1)S(1)}, u32[]{:S(2)}, u32[]{:S(2)}) collective-permute-start(bf16[128,1024]{1,0:T(8,128)(2,1)S(1)} %get-tuple-element.71), channel_id=1, source_target_pairs={{2,4},{6,8},{10,12},{14,0},{4,2},{8,6},{12,10},{0,14},{3,5},{7,9},... | collective-permute-start | bytes 786440 | tf_op jit(solution)/shard_map/ppermute | solution.py:309
  81.3 0.9 shard_map.86
  82.1 3.0 %collective-permute-start.10 = (bf16[128,1024]{1,0:T(8,128)(2,1)S(1)}, bf16[128,1024]{1,0:T(8,128)(2,1)S(1)}, u32[]{:S(2)}, u32[]{:S(2)}) collective-permute-start(bf16[128,1024]{1,0:T(8,128)(2,1)S(1)} %get-tuple-element.61), channel_id=1, source_target_pairs={{16,32},{48,64},{80,96},{112,128},{144,160},{176,192},{208,224},{2... | collective-permute-start | bytes 786440 | tf_op jit(solution)/shard_map/ppermute | solution.py:309
  85.2 0.5 collective-permute-done.23.rest_1_
  85.7 5.6 %collective-permute-start.12 = (bf16[128,1024]{1,0:T(8,128)(2,1)S(1)}, bf16[128,1024]{1,0:T(8,128)(2,1)S(1)}, u32[]{:S(2)}, u32[]{:S(2)}) collective-permute-start(bf16[128,1024]{1,0:T(8,128)(2,1)S(1)} %get-tuple-element.61), channel_id=1, source_target_pairs={{2,4},{6,8},{10,12},{14,0},{4,2},{8,6},{12,10},{0,14},{3,5},{7,9},... | collective-permute-start | bytes 786440 | tf_op jit(solution)/shard_map/ppermute | solution.py:309
  91.3 1.4 shard_map.90
  92.8 1.5 %collective-permute-start.26 = (bf16[128,1024]{1,0:T(8,128)(2,1)S(1)}, bf16[128,1024]{1,0:T(8,128)(2,1)S(1)}, u32[]{:S(2)}, u32[]{:S(2)}) collective-permute-start(bf16[128,1024]{1,0:T(8,128)(2,1)S(1)} %get-tuple-element.73), channel_id=1, source_target_pairs={{0,16},{32,48},{64,80},{96,112},{128,144},{160,176},{192,208},{224... | collective-permute-start | bytes 786440 | tf_op jit(solution)/shard_map/ppermute | solution.py:309
  94.3 1.1 collective-permute-start.27
  95.4 2.7 %collective-permute-start.29 = (bf16[128,1024]{1,0:T(8,128)(2,1)S(1)}, bf16[128,1024]{1,0:T(8,128)(2,1)S(1)}, u32[]{:S(2)}, u32[]{:S(2)}) collective-permute-start(bf16[128,1024]{1,0:T(8,128)(2,1)S(1)} %get-tuple-element.73), channel_id=1, source_target_pairs={{2,4},{6,8},{10,12},{14,0},{4,2},{8,6},{12,10},{0,14},{3,5},{7,9},... | collective-permute-start | bytes 786440 | tf_op jit(solution)/shard_map/ppermute | solution.py:309
  98.1 1.4 %shard_map.87 = (f32[128,1024]{1,0:T(8,128)S(1)}, bf16[128,1024]{1,0:T(8,128)(2,1)S(1)}) custom-call(s32[12]{0:T(128)S(1)} %stack.51.table_ref, f32[128,1024]{1,0:T(8,128)S(1)} %get-tuple-element.59.right_ref, f32[128,1024]{1,0:T(8,128)S(1)} %get-tuple-element.60.mine_ref, bf16[128,1024]{1,0:T(8,128)(2,1)S(1)} %collective-permute-done.9.rest_0_, ...), custom_call_target="tpu_custom_call" | custom-call | flops 268435456 | bytes 5242880 | tf_op jit(solution)/shard_map/pallas_call | solution.py:259
  99.5 0.3 collective-permute-start.13
  99.8 1.9 %collective-permute-done.26.rest_0_ = bf16[128,1024]{1,0:T(8,128)(2,1)S(1)} collective-permute-done((bf16[128,1024]{1,0:T(8,128)(2,1)S(1)}, bf16[128,1024]{1,0:T(8,128)(2,1)S(1)}, u32[]{:S(2)}, u32[]{:S(2)}) %collective-permute-start.26) | collective-permute-done | bytes 262176 | tf_op jit(solution)/shard_map/ppermute | solution.py:309
  101.7 0.7 collective-permute-start.14
  102.4 0.4 collective-permute-done.27.rest_1_
  103.0 1.3 collective-permute-start.16
  104.3 2.3 %shard_map.91 = (f32[2,1024,128]{2,1,0:T(8,128)}, f32[16,8,128]{2,1,0:T(8,128)S(1)}) custom-call(s32[12]{0:T(128)S(1)} %stack.51.table_ref, f32[128,1024]{1,0:T(8,128)S(1)} %get-tuple-element.69.right_ref, f32[128,1024]{1,0:T(8,128)S(1)} %get-tuple-element.72.mine_ref, bf16[128,1024]{1,0:T(8,128)(2,1)S(1)} %collective-permute-done.26.rest_0_, ...), custom_call_target="tpu_custom_call" | custom-call | flops 268435456 | bytes 5242880 | tf_op jit(solution)/shard_map/pallas_call | solution.py:286
  106.6 1.6 %collective-permute-done.13.rest_0_ = bf16[128,1024]{1,0:T(8,128)(2,1)S(1)} collective-permute-done((bf16[128,1024]{1,0:T(8,128)(2,1)S(1)}, bf16[128,1024]{1,0:T(8,128)(2,1)S(1)}, u32[]{:S(2)}, u32[]{:S(2)}) %collective-permute-start.13) | collective-permute-done | bytes 262176 | tf_op jit(solution)/shard_map/ppermute | solution.py:309
  108.1 2.5 %collective-permute-done.14.rest_1_ = bf16[128,1024]{1,0:T(8,128)(2,1)S(1)} collective-permute-done((bf16[128,1024]{1,0:T(8,128)(2,1)S(1)}, bf16[128,1024]{1,0:T(8,128)(2,1)S(1)}, u32[]{:S(2)}, u32[]{:S(2)}) %collective-permute-start.14) | collective-permute-done | bytes 262176 | tf_op jit(solution)/shard_map/ppermute | solution.py:309
  110.7 0.2 collective-permute-done.16.rest_3_
  110.9 2.2 %shard_map.92 = (f32[2,1024,128]{2,1,0:T(8,128)}, f32[16,8,128]{2,1,0:T(8,128)S(1)}) custom-call(s32[12]{0:T(128)S(1)} %stack.51.table_ref, f32[128,1024]{1,0:T(8,128)S(1)} %get-tuple-element.59.right_ref, f32[128,1024]{1,0:T(8,128)S(1)} %get-tuple-element.62.mine_ref, ...), custom_call_target="tpu_custom_call", output_to_operand_aliasing={{0}: (9, {})} | custom-call | flops 268435456 | bytes 5242880 | tf_op jit(solution)/shard_map/pallas_call | solution.py:286
  113.1 19.6 %all_to_all.10 = f32[16,8,128]{2,1,0:T(8,128)S(1)} all-to-all(f32[16,8,128]{2,1,0:T(8,128)S(1)} %get-tuple-element.77), channel_id=1, replica_groups=mesh['sx_0'=4,'sx_1'=4,'sy'=8,'freq'=2] {'sy','freq'}, dimensions={0} | all-to-all | bytes 131072 | tf_op jit(solution)/shard_map/all_to_all | solution.py:374
  132.7 9.6 %all_to_all.11 = f32[16,8,128]{2,1,0:T(8,128)S(1)} all-to-all(f32[16,8,128]{2,1,0:T(8,128)S(1)} %broadcast_in_dim.7), channel_id=1, replica_groups=mesh['sx_0'=4,'sx_1'=4,'sy'=8,'freq'=2] {'sx_0','sx_1'}, dimensions={0} | all-to-all | bytes 131072 | tf_op jit(solution)/shard_map/all_to_all | solution.py:376
  142.3 0.5 slice.3
  (47 shorter events, 1.0 us)
Async XLA Ops:
  0.6 12.7 %copy-start.2 = (bf16[2,32,32,128]{3,2,1,0:T(8,128)(2,1)S(1)}, bf16[2,32,32,128]{3,2,1,0:T(8,128)(2,1)}, u32[]{:S(2)}) copy-start(bf16[2,32,32,128]{3,2,1,0:T(8,128)(2,1)} %coeff_ref.5) | copy-start | bytes 1572868
  0.8 12.6 %copy-start = (bf16[2,32,32,1024]{3,2,1,0:T(8,128)(2,1)S(1)}, bf16[2,32,32,1024]{3,2,1,0:T(8,128)(2,1)}, u32[]{:S(2)}) copy-start(bf16[2,32,32,1024]{3,2,1,0:T(8,128)(2,1)} %basis_ref.5) | copy-start | bytes 12582916
  0.8 0.8 copy-start.5
  7.1 14.3 %collective-permute-start.3 = (bf16[2,128,1024]{2,1,0:T(8,128)(2,1)}, bf16[2,128,1024]{2,1,0:T(8,128)(2,1)S(1)}, u32[]{:S(2)}, u32[]{:S(2)}) collective-permute-start(bf16[2,128,1024]{2,1,0:T(8,128)(2,1)} %get-tuple-element.51), channel_id=1, source_target_pairs={{0,48},{16,0},{32,16},{48,32},{1,49},{17,1},{33,17},{49,33},{2,50}... | collective-permute-start | bytes 1572872 | tf_op jit(solution)/shard_map/ppermute | solution.py:304
  10.4 14.4 %collective-permute-start.2 = (bf16[2,128,1024]{2,1,0:T(8,128)(2,1)}, bf16[2,128,1024]{2,1,0:T(8,128)(2,1)S(1)}, u32[]{:S(2)}, u32[]{:S(2)}) collective-permute-start(bf16[2,128,1024]{2,1,0:T(8,128)(2,1)} %get-tuple-element.48), channel_id=1, source_target_pairs={{0,16},{16,32},{32,48},{48,0},{1,17},{17,33},{33,49},{49,1},{2,18}... | collective-permute-start | bytes 1572872 | tf_op jit(solution)/shard_map/ppermute | solution.py:304
  10.4 14.6 %collective-permute-start.1 = (bf16[2,128,1024]{2,1,0:T(8,128)(2,1)}, bf16[2,128,1024]{2,1,0:T(8,128)(2,1)S(1)}, u32[]{:S(2)}, u32[]{:S(2)}) collective-permute-start(bf16[2,128,1024]{2,1,0:T(8,128)(2,1)} %get-tuple-element.45), channel_id=1, source_target_pairs={{0,192},{64,0},{128,64},{192,128},{1,193},{65,1},{129,65},{193,129... | collective-permute-start | bytes 1572872 | tf_op jit(solution)/shard_map/ppermute | solution.py:304
  13.3 14.8 %collective-permute-start = (bf16[2,128,1024]{2,1,0:T(8,128)(2,1)S(1)}, bf16[2,128,1024]{2,1,0:T(8,128)(2,1)S(1)}, u32[]{:S(2)}, u32[]{:S(2)}) collective-permute-start(bf16[2,128,1024]{2,1,0:T(8,128)(2,1)S(1)} %get-tuple-element.42), channel_id=1, source_target_pairs={{0,64},{64,128},{128,192},{192,0},{1,65},{65,129},{129,193},{193,1... | collective-permute-start | bytes 1572872 | tf_op jit(solution)/shard_map/ppermute | solution.py:304
  21.5 24.4 %collective-permute-start.18 = (bf16[4,128,1024]{2,1,0:T(8,128)(2,1)S(1)}, bf16[4,128,1024]{2,1,0:T(8,128)(2,1)S(1)}, u32[]{:S(2)}, u32[]{:S(2)}) collective-permute-start(bf16[4,128,1024]{2,1,0:T(8,128)(2,1)S(1)} %shard_map.83.rest_3_), channel_id=1, source_target_pairs={{0,48},{16,0},{32,16},{48,32},{1,49},{17,1},{33,17},{49,33},{2,50}... | collective-permute-start | bytes 3145736 | tf_op jit(solution)/shard_map/ppermute | solution.py:304
  24.9 24.2 %collective-permute-start.17 = (bf16[4,128,1024]{2,1,0:T(8,128)(2,1)S(1)}, bf16[4,128,1024]{2,1,0:T(8,128)(2,1)S(1)}, u32[]{:S(2)}, u32[]{:S(2)}) collective-permute-start(bf16[4,128,1024]{2,1,0:T(8,128)(2,1)S(1)} %shard_map.82.rest_2_), channel_id=1, source_target_pairs={{0,16},{16,32},{32,48},{48,0},{1,17},{17,33},{33,49},{49,1},{2,18}... | collective-permute-start | bytes 3145736 | tf_op jit(solution)/shard_map/ppermute | solution.py:304
  25.1 28.6 %collective-permute-start.5 = (bf16[4,128,1024]{2,1,0:T(8,128)(2,1)S(1)}, bf16[4,128,1024]{2,1,0:T(8,128)(2,1)S(1)}, u32[]{:S(2)}, u32[]{:S(2)}) collective-permute-start(bf16[4,128,1024]{2,1,0:T(8,128)(2,1)S(1)} %shard_map.81.rest_1_), channel_id=1, source_target_pairs={{0,192},{64,0},{128,64},{192,128},{1,193},{65,1},{129,65},{193,129... | collective-permute-start | bytes 3145736 | tf_op jit(solution)/shard_map/ppermute | solution.py:304
  28.2 25.6 %collective-permute-start.4 = (bf16[4,128,1024]{2,1,0:T(8,128)(2,1)S(1)}, bf16[4,128,1024]{2,1,0:T(8,128)(2,1)S(1)}, u32[]{:S(2)}, u32[]{:S(2)}) collective-permute-start(bf16[4,128,1024]{2,1,0:T(8,128)(2,1)S(1)} %shard_map.80.rest_0_), channel_id=1, source_target_pairs={{0,64},{64,128},{128,192},{192,0},{1,65},{65,129},{129,193},{193,1... | collective-permute-start | bytes 3145736 | tf_op jit(solution)/shard_map/ppermute | solution.py:304
  49.1 20.6 %copy-start.1 = (bf16[2,1,1,1024,1024]{4,3,2,1,0:T(8,128)(2,1)S(1)}, bf16[2,1,1,1024,1024]{4,3,2,1,0:T(8,128)(2,1)}, u32[]{:S(2)}) copy-start(bf16[2,1,1,1024,1024]{4,3,2,1,0:T(8,128)(2,1)} %param.11) | copy-start | bytes 12582916
  49.1 20.6 %copy-start.4 = (bf16[2,1,1,1024,128]{4,3,2,1,0:T(8,128)(2,1)S(1)}, bf16[2,1,1,1024,128]{4,3,2,1,0:T(8,128)(2,1)}, u32[]{:S(2)}) copy-start(bf16[2,1,1,1024,128]{4,3,2,1,0:T(8,128)(2,1)} %param.9) | copy-start | bytes 1572868
  49.4 20.8 %collective-permute-start.20 = (f32[128,1024]{1,0:T(8,128)S(1)}, f32[128,1024]{1,0:T(8,128)S(1)}, u32[]{:S(2)}, u32[]{:S(2)}) collective-permute-start(f32[128,1024]{1,0:T(8,128)S(1)} %get-tuple-element.67), channel_id=1, source_target_pairs={{0,64},{64,128},{128,192},{192,0},{1,65},{65,129},{129,193},{193,1... | collective-permute-start | bytes 1572872 | tf_op jit(solution)/shard_map/ppermute | solution.py:304
  50.9 19.4 %collective-permute-start.21 = (f32[128,1024]{1,0:T(8,128)S(1)}, f32[128,1024]{1,0:T(8,128)S(1)}, u32[]{:S(2)}, u32[]{:S(2)}) collective-permute-start(f32[128,1024]{1,0:T(8,128)S(1)} %get-tuple-element.68), channel_id=1, source_target_pairs={{0,192},{64,0},{128,64},{192,128},{1,193},{65,1},{129,65},{193,129... | collective-permute-start | bytes 1572872 | tf_op jit(solution)/shard_map/ppermute | solution.py:304
  52.5 15.8 %collective-permute-start.19 = (bf16[128,1024]{1,0:T(8,128)(2,1)S(1)}, bf16[128,1024]{1,0:T(8,128)(2,1)S(1)}, u32[]{:S(2)}, u32[]{:S(2)}) collective-permute-start(bf16[128,1024]{1,0:T(8,128)(2,1)S(1)} %get-tuple-element.66), channel_id=1, source_target_pairs={{0,128},{64,192},{128,0},{192,64},{1,129},{65,193},{129,1},{193,65... | collective-permute-start | bytes 786440 | tf_op jit(solution)/shard_map/ppermute | solution.py:304
  54.1 22.5 %collective-permute-start.7 = (f32[128,1024]{1,0:T(8,128)S(1)}, f32[128,1024]{1,0:T(8,128)S(1)}, u32[]{:S(2)}, u32[]{:S(2)}) collective-permute-start(f32[128,1024]{1,0:T(8,128)S(1)} %get-tuple-element.56), channel_id=1, source_target_pairs={{0,16},{16,32},{32,48},{48,0},{1,17},{17,33},{33,49},{49,1},{2,18}... | collective-permute-start | bytes 1572872 | tf_op jit(solution)/shard_map/ppermute | solution.py:304
  54.2 27.1 %collective-permute-start.8 = (f32[128,1024]{1,0:T(8,128)S(1)}, f32[128,1024]{1,0:T(8,128)S(1)}, u32[]{:S(2)}, u32[]{:S(2)}) collective-permute-start(f32[128,1024]{1,0:T(8,128)S(1)} %get-tuple-element.57), channel_id=1, source_target_pairs={{0,48},{16,0},{32,16},{48,32},{1,49},{17,1},{33,17},{49,33},{2,50}... | collective-permute-start | bytes 1572872 | tf_op jit(solution)/shard_map/ppermute | solution.py:304
  68.2 6.7 %collective-permute-start.6 = (bf16[128,1024]{1,0:T(8,128)(2,1)S(1)}, bf16[128,1024]{1,0:T(8,128)(2,1)S(1)}, u32[]{:S(2)}, u32[]{:S(2)}) collective-permute-start(bf16[128,1024]{1,0:T(8,128)(2,1)S(1)} %get-tuple-element.55), channel_id=1, source_target_pairs={{0,32},{16,48},{32,0},{48,16},{1,33},{17,49},{33,1},{49,17},{2,34}... | collective-permute-start | bytes 786440 | tf_op jit(solution)/shard_map/ppermute | solution.py:304
  71.1 20.2 %copy-start.3 = (f32[2,1,1,4,1024]{4,3,2,1,0:T(4,128)S(1)}, f32[2,1,1,4,1024]{4,3,2,1,0:T(4,128)}, u32[]{:S(2)}) copy-start(f32[2,1,1,4,1024]{4,3,2,1,0:T(4,128)} %param.10) | copy-start | bytes 98308
  71.1 14.1 %collective-permute-start.22 = (bf16[128,1024]{1,0:T(8,128)(2,1)S(1)}, bf16[128,1024]{1,0:T(8,128)(2,1)S(1)}, u32[]{:S(2)}, u32[]{:S(2)}) collective-permute-start(bf16[128,1024]{1,0:T(8,128)(2,1)S(1)} %get-tuple-element.71), channel_id=1, source_target_pairs={{0,16},{32,48},{64,80},{96,112},{128,144},{160,176},{192,208},{224... | collective-permute-start | bytes 786440 | tf_op jit(solution)/shard_map/ppermute | solution.py:309
  73.2 12.5 %collective-permute-start.23 = (bf16[128,1024]{1,0:T(8,128)(2,1)S(1)}, bf16[128,1024]{1,0:T(8,128)(2,1)S(1)}, u32[]{:S(2)}, u32[]{:S(2)}) collective-permute-start(bf16[128,1024]{1,0:T(8,128)(2,1)S(1)} %get-tuple-element.71), channel_id=1, source_target_pairs={{16,32},{48,64},{80,96},{112,128},{144,160},{176,192},{208,224},{2... | collective-permute-start | bytes 786440 | tf_op jit(solution)/shard_map/ppermute | solution.py:309
  75.0 16.3 %collective-permute-start.24 = (bf16[128,1024]{1,0:T(8,128)(2,1)S(1)}, bf16[128,1024]{1,0:T(8,128)(2,1)S(1)}, u32[]{:S(2)}, u32[]{:S(2)}) collective-permute-start(bf16[128,1024]{1,0:T(8,128)(2,1)S(1)} %get-tuple-element.71), channel_id=1, source_target_pairs={{0,2},{4,6},{8,10},{12,14},{2,0},{6,4},{10,8},{14,12},{1,3},{5,7},... | collective-permute-start | bytes 786440 | tf_op jit(solution)/shard_map/ppermute | solution.py:309
  76.6 14.7 %collective-permute-start.25 = (bf16[128,1024]{1,0:T(8,128)(2,1)S(1)}, bf16[128,1024]{1,0:T(8,128)(2,1)S(1)}, u32[]{:S(2)}, u32[]{:S(2)}) collective-permute-start(bf16[128,1024]{1,0:T(8,128)(2,1)S(1)} %get-tuple-element.71), channel_id=1, source_target_pairs={{2,4},{6,8},{10,12},{14,0},{4,2},{8,6},{12,10},{0,14},{3,5},{7,9},... | collective-permute-start | bytes 786440 | tf_op jit(solution)/shard_map/ppermute | solution.py:309
  82.1 12.2 %collective-permute-start.10 = (bf16[128,1024]{1,0:T(8,128)(2,1)S(1)}, bf16[128,1024]{1,0:T(8,128)(2,1)S(1)}, u32[]{:S(2)}, u32[]{:S(2)}) collective-permute-start(bf16[128,1024]{1,0:T(8,128)(2,1)S(1)} %get-tuple-element.61), channel_id=1, source_target_pairs={{16,32},{48,64},{80,96},{112,128},{144,160},{176,192},{208,224},{2... | collective-permute-start | bytes 786440 | tf_op jit(solution)/shard_map/ppermute | solution.py:309
  85.2 10.2 %collective-permute-start.11 = (bf16[128,1024]{1,0:T(8,128)(2,1)S(1)}, bf16[128,1024]{1,0:T(8,128)(2,1)S(1)}, u32[]{:S(2)}, u32[]{:S(2)}) collective-permute-start(bf16[128,1024]{1,0:T(8,128)(2,1)S(1)} %get-tuple-element.61), channel_id=1, source_target_pairs={{0,2},{4,6},{8,10},{12,14},{2,0},{6,4},{10,8},{14,12},{1,3},{5,7},... | collective-permute-start | bytes 786440 | tf_op jit(solution)/shard_map/ppermute | solution.py:309
  85.7 9.6 %collective-permute-start.12 = (bf16[128,1024]{1,0:T(8,128)(2,1)S(1)}, bf16[128,1024]{1,0:T(8,128)(2,1)S(1)}, u32[]{:S(2)}, u32[]{:S(2)}) collective-permute-start(bf16[128,1024]{1,0:T(8,128)(2,1)S(1)} %get-tuple-element.61), channel_id=1, source_target_pairs={{2,4},{6,8},{10,12},{14,0},{4,2},{8,6},{12,10},{0,14},{3,5},{7,9},... | collective-permute-start | bytes 786440 | tf_op jit(solution)/shard_map/ppermute | solution.py:309
  91.3 6.8 %collective-permute-start.9 = (bf16[128,1024]{1,0:T(8,128)(2,1)S(1)}, bf16[128,1024]{1,0:T(8,128)(2,1)S(1)}, u32[]{:S(2)}, u32[]{:S(2)}) collective-permute-start(bf16[128,1024]{1,0:T(8,128)(2,1)S(1)} %get-tuple-element.61), channel_id=1, source_target_pairs={{0,16},{32,48},{64,80},{96,112},{128,144},{160,176},{192,208},{224... | collective-permute-start | bytes 786440 | tf_op jit(solution)/shard_map/ppermute | solution.py:309
  92.8 9.0 %collective-permute-start.26 = (bf16[128,1024]{1,0:T(8,128)(2,1)S(1)}, bf16[128,1024]{1,0:T(8,128)(2,1)S(1)}, u32[]{:S(2)}, u32[]{:S(2)}) collective-permute-start(bf16[128,1024]{1,0:T(8,128)(2,1)S(1)} %get-tuple-element.73), channel_id=1, source_target_pairs={{0,16},{32,48},{64,80},{96,112},{128,144},{160,176},{192,208},{224... | collective-permute-start | bytes 786440 | tf_op jit(solution)/shard_map/ppermute | solution.py:309
  94.3 8.5 %collective-permute-start.27 = (bf16[128,1024]{1,0:T(8,128)(2,1)S(1)}, bf16[128,1024]{1,0:T(8,128)(2,1)S(1)}, u32[]{:S(2)}, u32[]{:S(2)}) collective-permute-start(bf16[128,1024]{1,0:T(8,128)(2,1)S(1)} %get-tuple-element.73), channel_id=1, source_target_pairs={{16,32},{48,64},{80,96},{112,128},{144,160},{176,192},{208,224},{2... | collective-permute-start | bytes 786440 | tf_op jit(solution)/shard_map/ppermute | solution.py:309
  95.4 7.6 %collective-permute-start.28 = (bf16[128,1024]{1,0:T(8,128)(2,1)S(1)}, bf16[128,1024]{1,0:T(8,128)(2,1)S(1)}, u32[]{:S(2)}, u32[]{:S(2)}) collective-permute-start(bf16[128,1024]{1,0:T(8,128)(2,1)S(1)} %get-tuple-element.73), channel_id=1, source_target_pairs={{0,2},{4,6},{8,10},{12,14},{2,0},{6,4},{10,8},{14,12},{1,3},{5,7},... | collective-permute-start | bytes 786440 | tf_op jit(solution)/shard_map/ppermute | solution.py:309
  95.4 8.9 %collective-permute-start.29 = (bf16[128,1024]{1,0:T(8,128)(2,1)S(1)}, bf16[128,1024]{1,0:T(8,128)(2,1)S(1)}, u32[]{:S(2)}, u32[]{:S(2)}) collective-permute-start(bf16[128,1024]{1,0:T(8,128)(2,1)S(1)} %get-tuple-element.73), channel_id=1, source_target_pairs={{2,4},{6,8},{10,12},{14,0},{4,2},{8,6},{12,10},{0,14},{3,5},{7,9},... | collective-permute-start | bytes 786440 | tf_op jit(solution)/shard_map/ppermute | solution.py:309
  99.5 8.6 %collective-permute-start.13 = (bf16[128,1024]{1,0:T(8,128)(2,1)S(1)}, bf16[128,1024]{1,0:T(8,128)(2,1)S(1)}, u32[]{:S(2)}, u32[]{:S(2)}) collective-permute-start(bf16[128,1024]{1,0:T(8,128)(2,1)S(1)} %get-tuple-element.63), channel_id=1, source_target_pairs={{0,16},{32,48},{64,80},{96,112},{128,144},{160,176},{192,208},{224... | collective-permute-start | bytes 786440 | tf_op jit(solution)/shard_map/ppermute | solution.py:309
  101.7 9.0 %collective-permute-start.14 = (bf16[128,1024]{1,0:T(8,128)(2,1)S(1)}, bf16[128,1024]{1,0:T(8,128)(2,1)S(1)}, u32[]{:S(2)}, u32[]{:S(2)}) collective-permute-start(bf16[128,1024]{1,0:T(8,128)(2,1)S(1)} %get-tuple-element.63), channel_id=1, source_target_pairs={{16,32},{48,64},{80,96},{112,128},{144,160},{176,192},{208,224},{2... | collective-permute-start | bytes 786440 | tf_op jit(solution)/shard_map/ppermute | solution.py:309
  102.8 7.8 %collective-permute-start.15 = (bf16[128,1024]{1,0:T(8,128)(2,1)S(1)}, bf16[128,1024]{1,0:T(8,128)(2,1)S(1)}, u32[]{:S(2)}, u32[]{:S(2)}) collective-permute-start(bf16[128,1024]{1,0:T(8,128)(2,1)S(1)} %get-tuple-element.63), channel_id=1, source_target_pairs={{0,2},{4,6},{8,10},{12,14},{2,0},{6,4},{10,8},{14,12},{1,3},{5,7},... | collective-permute-start | bytes 786440 | tf_op jit(solution)/shard_map/ppermute | solution.py:309
  103.0 7.9 %collective-permute-start.16 = (bf16[128,1024]{1,0:T(8,128)(2,1)S(1)}, bf16[128,1024]{1,0:T(8,128)(2,1)S(1)}, u32[]{:S(2)}, u32[]{:S(2)}) collective-permute-start(bf16[128,1024]{1,0:T(8,128)(2,1)S(1)} %get-tuple-element.63), channel_id=1, source_target_pairs={{2,4},{6,8},{10,12},{14,0},{4,2},{8,6},{12,10},{0,14},{3,5},{7,9},... | collective-permute-start | bytes 786440 | tf_op jit(solution)/shard_map/ppermute | solution.py:309
where the time goes:
time: 145 us
  starting transfers between devices  46.4 us (32%)
  waiting for transfers between devices  44.7 us (31%)
  blocking collectives  29.2 us (20%)
  Pallas kernels  20.2 us (14%)
  between operations  2.7 us (2%)
    ppermute x14, waiting for transfers between devices, turn(): return lax.ppermute(x, axis, [(i, (i + by) % SIDE) for i in range(SIDE)])  37.5 us
    ppermute x16, starting transfers between devices, neighbours(): lax.ppermute(x, axis, p + [(b, a) for a, b in p])  25.1 us
    ppermute x14, starting transfers between devices, turn(): return lax.ppermute(x, axis, [(i, (i + by) % SIDE) for i in range(SIDE)])  21.3 us
    all_to_all x1, blocking collectives, on_device(): squares = jnp.sum(lax.all_to_all(squares, group, 0, 0, tiled=True), axis=0)  19.6 us
    pallas_call x3, Pallas kernels, owner_products(): pl.pallas_call(body, in_specs=[pl.BlockSpec(memory_space=pltpu.MemorySpac...  9.74 us
    all_to_all x1, blocking collectives, on_device(): squares = jnp.sum(lax.all_to_all(squares, SX, 0, 0, tiled=True), axis=0)  9.61 us
    ppermute x16, waiting for transfers between devices, neighbours(): lax.ppermute(x, axis, p + [(b, a) for a, b in p])  7.16 us
    pallas_call x2, Pallas kernels, last_sweep(): pl.pallas_call(body, grid=(1,), in_specs=[pl.BlockSpec(memory_space=pltpu...  4.49 us
  transfers between devices with their start and end apart: 30, of which 11 were waited for; matrix products, arithmetic and copies ran while one was open for 0% of the time, Pallas kernels for 9%

commit v1 on v0

--- a/solution.py
+++ b/solution.py
@@ -11,6 +11,7 @@
 SIDE = 4
 CAP = 4
 TILE = 256
+SPARE = 16
 SX = ("sx_0", "sx_1")
 SX_SY = ("sx_0", "sx_1", "sy")
 LOW, HIGH = (0, 1), (3, 2)
@@ -160,18 +161,29 @@
 def row_totals(own, low, high):
     _, rhs_count, sep_size = own.shape
 
-    def body(own_ref, low_ref, high_ref, *outs):
-        for at, out in enumerate(outs):
+    def body(own_ref, low_ref, high_ref, here, following, preceding, opposite):
+        def total(at):
             crossed = (at + 2) % SIDE
-            total = own_ref[at] + low_ref[at].astype(jnp.float32) + high_ref[crossed].astype(jnp.float32)
-            out[...] = total.astype(out.dtype)
-
-    types = (jnp.float32,) * 3 + (jnp.bfloat16,)
+            return own_ref[at] + low_ref[at].astype(jnp.float32) + high_ref[crossed].astype(jnp.float32)
+
+        here[...] = total(0)
+        for at, out in ((1, following), (2, preceding)):
+            sums = total(at)
+            largest = jnp.max(jnp.abs(sums), axis=0, keepdims=True)
+            largest = jnp.broadcast_to(jnp.max(largest), (SPARE, sep_size))
+            power = jnp.clip(14.0 - jnp.ceil(jnp.log2(largest)), -60.0, 100.0)
+            out[:rhs_count] = sums * jnp.exp2(power[:1])
+            out[rhs_count:] = power
+        opposite[...] = total(3).astype(jnp.bfloat16)
+
+    plain = (rhs_count, sep_size)
+    wide = (rhs_count + SPARE, sep_size)
     return pl.pallas_call(
         body,
         in_specs=in_vmem(3),
         out_specs=in_vmem(SIDE),
-        out_shape=[jax.ShapeDtypeStruct((rhs_count, sep_size), dtype) for dtype in types],
+        out_shape=[jax.ShapeDtypeStruct(shape, jnp.float32) for shape in (plain, wide, wide)]
+        + [jax.ShapeDtypeStruct(plain, jnp.bfloat16)],
         compiler_params=room(4),
         cost_estimate=cost(own.size * 2, own.size * 12),
     )(own, low, high)
@@ -214,9 +226,10 @@
 
     def body(rhs_ref, *rest):
         parts_refs, (matrix_ref, right_ref, out_ref, sent_ref) = rest[:-4], rest[-4:]
-        right = rhs_ref[f]
-        for part in parts_refs:
-            right = right - part[...].astype(jnp.float32)
+        here, opposite, *beside = parts_refs
+        right = rhs_ref[f] - here[...] - opposite[...].astype(jnp.float32)
+        for part in beside:
+            right = right - part[:rhs_count] * jnp.exp2(-part[rhs_count : rhs_count + 1])
         right_ref[...] = right
         field = right.astype(jnp.bfloat16)
         for s in range(0, sep_size, TILE):
@@ -357,7 +370,11 @@
         here, following, preceding, opposite = row_totals(own[f], *sums[f])
         axis = axes[f][1]
         opposite = turn(opposite, axis, 2)
-        parts = (opposite, turn(following, axis, 1), turn(preceding, axis, -1))
+        beside = [
+            turn(sums_of.astype(jnp.float16), axis, by).astype(full)
+            for sums_of, by in ((following, 1), (preceding, -1))
+        ]
+        parts = (opposite, *beside)
         right_side[f], mine[f], sent[f] = first_solve(f, rhs, (here, *parts), matrix)
     for _ in range(SWEEPS - 1):
         for f in order:

time: 145 us -> 138 us (0.952)
  waiting for transfers between devices: 44.7 us -> 34.5 us
  starting transfers between devices: 46.4 us -> 48.9 us
    ppermute x14, waiting for transfers between devices: 37.5 us -> 28.6 us  [turn(): return lax.ppermute(x, axis, [(i, (i + by) % SIDE) for i in range(SIDE)])]
    ppermute x16, starting transfers between devices: 25.1 us -> 27.5 us  [neighbours(): lax.ppermute(x, axis, p + [(b, a) for a, b in p])]
  transfers between devices with their start and end apart: 30 -> 30, of which waited for: 11 -> 9; matrix products, arithmetic and copies ran while one was open for 0% -> 0% of each run, Pallas kernels for 9% -> 9%
where the time goes in v1:
time: 138 us
  starting transfers between devices  48.9 us (35%)
  waiting for transfers between devices  34.5 us (25%)
  blocking collectives  29.2 us (21%)
  Pallas kernels  20.8 us (15%)
  between operations  2.8 us (2%)
  local copies, waits for them, and re-layouts  1.44 us (1%)
    ppermute x14, waiting for transfers between devices, turn(): return lax.ppermute(x, axis, [(i, (i + by) % SIDE) for i in range(SIDE)])  28.6 us
    ppermute x16, starting transfers between devices, neighbours(): lax.ppermute(x, axis, p + [(b, a) for a, b in p])  27.5 us
    ppermute x14, starting transfers between devices, turn(): return lax.ppermute(x, axis, [(i, (i + by) % SIDE) for i in range(SIDE)])  21.4 us
    all_to_all x1, blocking collectives, on_device(): squares = jnp.sum(lax.all_to_all(squares, group, 0, 0, tiled=True), axis=0)  19 us
    all_to_all x1, blocking collectives, on_device(): squares = jnp.sum(lax.all_to_all(squares, SX, 0, 0, tiled=True), axis=0)  10.2 us
    pallas_call x3, Pallas kernels, owner_products(): pl.pallas_call(body, in_specs=[pl.BlockSpec(memory_space=pltpu.MemorySpac...  9.74 us
    ppermute x16, waiting for transfers between devices, neighbours(): lax.ppermute(x, axis, p + [(b, a) for a, b in p])  5.99 us
    pallas_call x2, Pallas kernels, last_sweep(): pl.pallas_call(body, grid=(1,), in_specs=[pl.BlockSpec(memory_space=pltpu...  4.49 us
  transfers between devices with their start and end apart: 30, of which 9 were waited for; matrix products, arithmetic and copies ran while one was open for 0% of the time, Pallas kernels for 9%

profile of v1, /device:TPU:1, one launch (start us, length us, event | category | flops | bytes accessed | tf_op | source)
XLA Modules:
  0.0 138.1 jit_solution(4440799349175550706)
XLA Ops:
  0.7 0.1 stack.51.table_ref
  0.8 0.8 copy-done.5
  1.6 5.5 %shard_map.79 = (bf16[2,128,1024]{2,1,0:T(8,128)(2,1)S(1)}, bf16[2,128,1024]{2,1,0:T(8,128)(2,1)}, bf16[2,128,1024]{2,1,0:T(8,128)(2,1)}, bf16[2,128,1024]{2,1,0:T(8,128)(2,1)}) custom-call(s32[32]{0:T(128)S(1)} %bitcast.24, s32[12]{0:T(128)S(1)} %stack.51.table_ref, bf16[2,32,32,1024]{3,2,1,0:T(8,128)(2,1)} %basis_ref.5, bf16[2,32,32,128]{3,2,1,0:T(8,128)(2,1)} %coeff_ref.5), custom_call_target="tpu_custom_call" | custom-call | flops 1073741824 | bytes 6291456 | tf_op jit(solution)/shard_map/pallas_call | solution.py:119
  7.1 3.3 %collective-permute-start.3 = (bf16[2,128,1024]{2,1,0:T(8,128)(2,1)}, bf16[2,128,1024]{2,1,0:T(8,128)(2,1)S(1)}, u32[]{:S(2)}, u32[]{:S(2)}) collective-permute-start(bf16[2,128,1024]{2,1,0:T(8,128)(2,1)} %get-tuple-element.51), channel_id=1, source_target_pairs={{0,48},{16,0},{32,16},{48,32},{1,49},{17,1},{33,17},{49,33},{2,50}... | collective-permute-start | bytes 1572872 | tf_op jit(solution)/shard_map/ppermute | solution.py:317
  10.4 2.9 %collective-permute-start.1 = (bf16[2,128,1024]{2,1,0:T(8,128)(2,1)}, bf16[2,128,1024]{2,1,0:T(8,128)(2,1)S(1)}, u32[]{:S(2)}, u32[]{:S(2)}) collective-permute-start(bf16[2,128,1024]{2,1,0:T(8,128)(2,1)} %get-tuple-element.45), channel_id=1, source_target_pairs={{0,192},{64,0},{128,64},{192,128},{1,193},{65,1},{129,65},{193,129... | collective-permute-start | bytes 1572872 | tf_op jit(solution)/shard_map/ppermute | solution.py:317
  13.3 2.4 %shard_map.78 = (f32[2,128,1024]{2,1,0:T(8,128)S(1)}, f32[2,128,1024]{2,1,0:T(8,128)S(1)}, f32[2,128,1024]{2,1,0:T(8,128)S(1)}, f32[2,128,1024]{2,1,0:T(8,128)S(...) custom-call(s32[32]{0:T(128)S(1)} %bitcast.25, ...), custom_call_target="tpu_custom_call" | custom-call | flops 2147483648 | bytes 12582912 | tf_op jit(solution)/shard_map/pallas_call | solution.py:119
  15.7 5.6 %collective-permute-done.3.got_ref = bf16[2,128,1024]{2,1,0:T(8,128)(2,1)S(1)} collective-permute-done((bf16[2,128,1024]{2,1,0:T(8,128)(2,1)}, bf16[2,128,1024]{2,1,0:T(8,128)(2,1)S(1)}, u32[]{:S(2)}, u32[]{:S(2)}) %collective-permute-start.3) | collective-permute-done | bytes 524320 | tf_op jit(solution)/shard_map/ppermute | solution.py:317
  21.5 3.4 %collective-permute-start.18 = (bf16[4,128,1024]{2,1,0:T(8,128)(2,1)S(1)}, bf16[4,128,1024]{2,1,0:T(8,128)(2,1)S(1)}, u32[]{:S(2)}, u32[]{:S(2)}) collective-permute-start(bf16[4,128,1024]{2,1,0:T(8,128)(2,1)S(1)} %shard_map.83.rest_3_), channel_id=1, source_target_pairs={{0,48},{16,0},{32,16},{48,32},{1,49},{17,1},{33,17},{49,33},{2,50}... | collective-permute-start | bytes 3145736 | tf_op jit(solution)/shard_map/ppermute | solution.py:317
  25.0 0.1 shard_map.81.rest_1_
  25.1 2.9 %collective-permute-start.5 = (bf16[4,128,1024]{2,1,0:T(8,128)(2,1)S(1)}, bf16[4,128,1024]{2,1,0:T(8,128)(2,1)S(1)}, u32[]{:S(2)}, u32[]{:S(2)}) collective-permute-start(bf16[4,128,1024]{2,1,0:T(8,128)(2,1)S(1)} %shard_map.81.rest_1_), channel_id=1, source_target_pairs={{0,192},{64,0},{128,64},{192,128},{1,193},{65,1},{129,65},{193,129... | collective-permute-start | bytes 3145736 | tf_op jit(solution)/shard_map/ppermute | solution.py:317
  28.3 1.8 %shard_map.84 = (f32[4,128,1024]{2,1,0:T(8,128)S(1)}, f32[4,128,1024]{2,1,0:T(8,128)S(1)}) custom-call(s32[32]{0:T(128)S(1)} %bitcast.26, s32[12]{0:T(128)S(1)} %stack.51.table_ref, bf16[2,32,32,1024]{3,2,1,0:T(8,128)(2,1)S(1)} %copy-done, bf16[2,32,32,128]{3,2,1,0:T(8,128)(2,1)S(1)} %copy-done.2, bf16[4,128,1024]{2,1,0:T(8,128)(2,1)S(1)} %shard_map.80.rest_0_, ...), custom_call_target="tpu_custom_call" | custom-call | flops 1073741824 | bytes 6291456 | tf_op jit(solution)/shard_map/pallas_call | solution.py:119
  30.1 15.7 %collective-permute-done.18.high_ref = bf16[4,128,1024]{2,1,0:T(8,128)(2,1)S(1)} collective-permute-done((bf16[4,128,1024]{2,1,0:T(8,128)(2,1)S(1)}, bf16[4,128,1024]{2,1,0:T(8,128)(2,1)S(1)}, u32[]{:S(2)}, u32[]{:S(2)}) %collective-permute-start.18) | collective-permute-done | bytes 1048608 | tf_op jit(solution)/shard_map/ppermute | solution.py:317
  45.8 3.3 %collective-permute-done.17.low_ref = bf16[4,128,1024]{2,1,0:T(8,128)(2,1)S(1)} collective-permute-done((bf16[4,128,1024]{2,1,0:T(8,128)(2,1)S(1)}, bf16[4,128,1024]{2,1,0:T(8,128)(2,1)S(1)}, u32[]{:S(2)}, u32[]{:S(2)}) %collective-permute-start.17) | collective-permute-done | bytes 1048608 | tf_op jit(solution)/shard_map/ppermute | solution.py:317
  49.1 0.6 shard_map.88
  49.8 1.4 %collective-permute-start.20 = (f16[144,1024]{1,0:T(8,128)(2,1)S(1)}, f16[144,1024]{1,0:T(8,128)(2,1)S(1)}, u32[]{:S(2)}, u32[]{:S(2)}) collective-permute-start(f16[144,1024]{1,0:T(8,128)(2,1)S(1)} %convert_element_type.30), channel_id=1, source_target_pairs={{0,64},{64,128},{128,192},{192,0},{1,65},{65,129},{129,193},{193,1... | collective-permute-start | bytes 884744 | tf_op jit(solution)/shard_map/ppermute | solution.py:317
  51.3 1.6 %collective-permute-start.21 = (f16[144,1024]{1,0:T(8,128)(2,1)S(1)}, f16[144,1024]{1,0:T(8,128)(2,1)S(1)}, u32[]{:S(2)}, u32[]{:S(2)}) collective-permute-start(f16[144,1024]{1,0:T(8,128)(2,1)S(1)} %convert_element_type.32), channel_id=1, source_target_pairs={{0,192},{64,0},{128,64},{192,128},{1,193},{65,1},{129,65},{193,129... | collective-permute-start | bytes 884744 | tf_op jit(solution)/shard_map/ppermute | solution.py:317
  52.9 1.4 %collective-permute-start.19 = (bf16[128,1024]{1,0:T(8,128)(2,1)S(1)}, bf16[128,1024]{1,0:T(8,128)(2,1)S(1)}, u32[]{:S(2)}, u32[]{:S(2)}) collective-permute-start(bf16[128,1024]{1,0:T(8,128)(2,1)S(1)} %get-tuple-element.66), channel_id=1, source_target_pairs={{0,128},{64,192},{128,0},{192,64},{1,129},{65,193},{129,1},{193,65... | collective-permute-start | bytes 786440 | tf_op jit(solution)/shard_map/ppermute | solution.py:317
  54.3 0.6 shard_map.85
  55.1 2.7 %collective-permute-start.8 = (f16[144,1024]{1,0:T(8,128)(2,1)S(1)}, f16[144,1024]{1,0:T(8,128)(2,1)S(1)}, u32[]{:S(2)}, u32[]{:S(2)}) collective-permute-start(f16[144,1024]{1,0:T(8,128)(2,1)S(1)} %convert_element_type.28), channel_id=1, source_target_pairs={{0,48},{16,0},{32,16},{48,32},{1,49},{17,1},{33,17},{49,33},{2,50}... | collective-permute-start | bytes 884744 | tf_op jit(solution)/shard_map/ppermute | solution.py:317
  57.9 0.4 shard_map.77
  58.3 0.7 collective-permute-done.20
  59.0 1.4 %collective-permute-start.6 = (bf16[128,1024]{1,0:T(8,128)(2,1)S(1)}, bf16[128,1024]{1,0:T(8,128)(2,1)S(1)}, u32[]{:S(2)}, u32[]{:S(2)}) collective-permute-start(bf16[128,1024]{1,0:T(8,128)(2,1)S(1)} %get-tuple-element.55), channel_id=1, source_target_pairs={{0,32},{16,48},{32,0},{48,16},{1,33},{17,49},{33,1},{49,17},{2,34}... | collective-permute-start | bytes 786440 | tf_op jit(solution)/shard_map/ppermute | solution.py:317
  60.5 3.2 %collective-permute-done.19.rest_1_ = bf16[128,1024]{1,0:T(8,128)(2,1)S(1)} collective-permute-done((bf16[128,1024]{1,0:T(8,128)(2,1)S(1)}, bf16[128,1024]{1,0:T(8,128)(2,1)S(1)}, u32[]{:S(2)}, u32[]{:S(2)}) %collective-permute-start.19) | collective-permute-done | bytes 262176 | tf_op jit(solution)/shard_map/ppermute | solution.py:317
  63.7 0.9 shard_map.89
  64.6 0.1 collective-permute-start.22
  64.7 1.2 collective-permute-start.23
  65.9 1.6 %collective-permute-start.24 = (bf16[128,1024]{1,0:T(8,128)(2,1)S(1)}, bf16[128,1024]{1,0:T(8,128)(2,1)S(1)}, u32[]{:S(2)}, u32[]{:S(2)}) collective-permute-start(bf16[128,1024]{1,0:T(8,128)(2,1)S(1)} %get-tuple-element.71), channel_id=1, source_target_pairs={{0,2},{4,6},{8,10},{12,14},{2,0},{6,4},{10,8},{14,12},{1,3},{5,7},... | collective-permute-start | bytes 786440 | tf_op jit(solution)/shard_map/ppermute | solution.py:322
  67.5 4.6 %collective-permute-start.25 = (bf16[128,1024]{1,0:T(8,128)(2,1)S(1)}, bf16[128,1024]{1,0:T(8,128)(2,1)S(1)}, u32[]{:S(2)}, u32[]{:S(2)}) collective-permute-start(bf16[128,1024]{1,0:T(8,128)(2,1)S(1)} %get-tuple-element.71), channel_id=1, source_target_pairs={{2,4},{6,8},{10,12},{14,0},{4,2},{8,6},{12,10},{0,14},{3,5},{7,9},... | collective-permute-start | bytes 786440 | tf_op jit(solution)/shard_map/ppermute | solution.py:322
  72.2 0.9 shard_map.86
  73.1 3.8 %collective-permute-start.10 = (bf16[128,1024]{1,0:T(8,128)(2,1)S(1)}, bf16[128,1024]{1,0:T(8,128)(2,1)S(1)}, u32[]{:S(2)}, u32[]{:S(2)}) collective-permute-start(bf16[128,1024]{1,0:T(8,128)(2,1)S(1)} %get-tuple-element.61), channel_id=1, source_target_pairs={{16,32},{48,64},{80,96},{112,128},{144,160},{176,192},{208,224},{2... | collective-permute-start | bytes 786440 | tf_op jit(solution)/shard_map/ppermute | solution.py:322
  76.9 4.0 %collective-permute-start.12 = (bf16[128,1024]{1,0:T(8,128)(2,1)S(1)}, bf16[128,1024]{1,0:T(8,128)(2,1)S(1)}, u32[]{:S(2)}, u32[]{:S(2)}) collective-permute-start(bf16[128,1024]{1,0:T(8,128)(2,1)S(1)} %get-tuple-element.61), channel_id=1, source_target_pairs={{2,4},{6,8},{10,12},{14,0},{4,2},{8,6},{12,10},{0,14},{3,5},{7,9},... | collective-permute-start | bytes 786440 | tf_op jit(solution)/shard_map/ppermute | solution.py:322
  81.0 1.4 %shard_map.90 = (f32[128,1024]{1,0:T(8,128)S(1)}, bf16[128,1024]{1,0:T(8,128)(2,1)S(1)}) custom-call(s32[12]{0:T(128)S(1)} %stack.51.table_ref, f32[128,1024]{1,0:T(8,128)S(1)} %get-tuple-element.69.right_ref, f32[128,1024]{1,0:T(8,128)S(1)} %get-tuple-element.70.mine_ref, bf16[128,1024]{1,0:T(8,128)(2,1)S(1)} %collective-permute-done.22.rest_0_, ...), custom_call_target="tpu_custom_call" | custom-call | flops 268435456 | bytes 5242880 | tf_op jit(solution)/shard_map/pallas_call | solution.py:272
  82.4 1.5 %collective-permute-start.26 = (bf16[128,1024]{1,0:T(8,128)(2,1)S(1)}, bf16[128,1024]{1,0:T(8,128)(2,1)S(1)}, u32[]{:S(2)}, u32[]{:S(2)}) collective-permute-start(bf16[128,1024]{1,0:T(8,128)(2,1)S(1)} %get-tuple-element.73), channel_id=1, source_target_pairs={{0,16},{32,48},{64,80},{96,112},{128,144},{160,176},{192,208},{224... | collective-permute-start | bytes 786440 | tf_op jit(solution)/shard_map/ppermute | solution.py:322
  83.9 4.2 %collective-permute-start.27 = (bf16[128,1024]{1,0:T(8,128)(2,1)S(1)}, bf16[128,1024]{1,0:T(8,128)(2,1)S(1)}, u32[]{:S(2)}, u32[]{:S(2)}) collective-permute-start(bf16[128,1024]{1,0:T(8,128)(2,1)S(1)} %get-tuple-element.73), channel_id=1, source_target_pairs={{16,32},{48,64},{80,96},{112,128},{144,160},{176,192},{208,224},{2... | collective-permute-start | bytes 786440 | tf_op jit(solution)/shard_map/ppermute | solution.py:322
  88.1 3.1 %collective-permute-start.29 = (bf16[128,1024]{1,0:T(8,128)(2,1)S(1)}, bf16[128,1024]{1,0:T(8,128)(2,1)S(1)}, u32[]{:S(2)}, u32[]{:S(2)}) collective-permute-start(bf16[128,1024]{1,0:T(8,128)(2,1)S(1)} %get-tuple-element.73), channel_id=1, source_target_pairs={{2,4},{6,8},{10,12},{14,0},{4,2},{8,6},{12,10},{0,14},{3,5},{7,9},... | collective-permute-start | bytes 786440 | tf_op jit(solution)/shard_map/ppermute | solution.py:322
  91.2 1.4 %shard_map.87 = (f32[128,1024]{1,0:T(8,128)S(1)}, bf16[128,1024]{1,0:T(8,128)(2,1)S(1)}) custom-call(s32[12]{0:T(128)S(1)} %stack.51.table_ref, f32[128,1024]{1,0:T(8,128)S(1)} %get-tuple-element.59.right_ref, f32[128,1024]{1,0:T(8,128)S(1)} %get-tuple-element.60.mine_ref, bf16[128,1024]{1,0:T(8,128)(2,1)S(1)} %collective-permute-done.9.rest_0_, ...), custom_call_target="tpu_custom_call" | custom-call | flops 268435456 | bytes 5242880 | tf_op jit(solution)/shard_map/pallas_call | solution.py:272
  92.7 0.1 collective-permute-start.13
  92.8 2.3 %collective-permute-start.14 = (bf16[128,1024]{1,0:T(8,128)(2,1)S(1)}, bf16[128,1024]{1,0:T(8,128)(2,1)S(1)}, u32[]{:S(2)}, u32[]{:S(2)}) collective-permute-start(bf16[128,1024]{1,0:T(8,128)(2,1)S(1)} %get-tuple-element.63), channel_id=1, source_target_pairs={{16,32},{48,64},{80,96},{112,128},{144,160},{176,192},{208,224},{2... | collective-permute-start | bytes 786440 | tf_op jit(solution)/shard_map/ppermute | solution.py:322
  95.2 0.9 collective-permute-start.16
  96.0 2.3 %shard_map.91 = (f32[2,1024,128]{2,1,0:T(8,128)}, f32[16,8,128]{2,1,0:T(8,128)S(1)}) custom-call(s32[12]{0:T(128)S(1)} %stack.51.table_ref, f32[128,1024]{1,0:T(8,128)S(1)} %get-tuple-element.69.right_ref, f32[128,1024]{1,0:T(8,128)S(1)} %get-tuple-element.72.mine_ref, bf16[128,1024]{1,0:T(8,128)(2,1)S(1)} %collective-permute-done.26.rest_0_, ...), custom_call_target="tpu_custom_call" | custom-call | flops 268435456 | bytes 5242880 | tf_op jit(solution)/shard_map/pallas_call | solution.py:299
  98.3 0.9 collective-permute-done.13.rest_0_
  99.2 3.8 %collective-permute-done.14.rest_1_ = bf16[128,1024]{1,0:T(8,128)(2,1)S(1)} collective-permute-done((bf16[128,1024]{1,0:T(8,128)(2,1)S(1)}, bf16[128,1024]{1,0:T(8,128)(2,1)S(1)}, u32[]{:S(2)}, u32[]{:S(2)}) %collective-permute-start.14) | collective-permute-done | bytes 262176 | tf_op jit(solution)/shard_map/ppermute | solution.py:322
  102.9 0.3 collective-permute-done.15.rest_2_
  103.2 1.1 collective-permute-done.16.rest_3_
  104.2 2.2 %shard_map.92 = (f32[2,1024,128]{2,1,0:T(8,128)}, f32[16,8,128]{2,1,0:T(8,128)S(1)}) custom-call(s32[12]{0:T(128)S(1)} %stack.51.table_ref, f32[128,1024]{1,0:T(8,128)S(1)} %get-tuple-element.59.right_ref, f32[128,1024]{1,0:T(8,128)S(1)} %get-tuple-element.62.mine_ref, ...), custom_call_target="tpu_custom_call", output_to_operand_aliasing={{0}: (9, {})} | custom-call | flops 268435456 | bytes 5242880 | tf_op jit(solution)/shard_map/pallas_call | solution.py:299
  106.5 19.0 %all_to_all.10 = f32[16,8,128]{2,1,0:T(8,128)S(1)} all-to-all(f32[16,8,128]{2,1,0:T(8,128)S(1)} %get-tuple-element.77), channel_id=1, replica_groups=mesh['sx_0'=4,'sx_1'=4,'sy'=8,'freq'=2] {'sy','freq'}, dimensions={0} | all-to-all | bytes 131072 | tf_op jit(solution)/shard_map/all_to_all | solution.py:391
  125.5 10.2 %all_to_all.11 = f32[16,8,128]{2,1,0:T(8,128)S(1)} all-to-all(f32[16,8,128]{2,1,0:T(8,128)S(1)} %broadcast_in_dim.7), channel_id=1, replica_groups=mesh['sx_0'=4,'sx_1'=4,'sy'=8,'freq'=2] {'sx_0','sx_1'}, dimensions={0} | all-to-all | bytes 131072 | tf_op jit(solution)/shard_map/all_to_all | solution.py:393
  135.8 0.5 slice.3
  (55 shorter events, 1.0 us)
Async XLA Ops:
  0.6 12.7 %copy-start.2 = (bf16[2,32,32,128]{3,2,1,0:T(8,128)(2,1)S(1)}, bf16[2,32,32,128]{3,2,1,0:T(8,128)(2,1)}, u32[]{:S(2)}) copy-start(bf16[2,32,32,128]{3,2,1,0:T(8,128)(2,1)} %coeff_ref.5) | copy-start | bytes 1572868
  0.8 12.6 %copy-start = (bf16[2,32,32,1024]{3,2,1,0:T(8,128)(2,1)S(1)}, bf16[2,32,32,1024]{3,2,1,0:T(8,128)(2,1)}, u32[]{:S(2)}) copy-start(bf16[2,32,32,1024]{3,2,1,0:T(8,128)(2,1)} %basis_ref.5) | copy-start | bytes 12582916
  0.8 0.8 copy-start.5
  7.1 14.3 %collective-permute-start.3 = (bf16[2,128,1024]{2,1,0:T(8,128)(2,1)}, bf16[2,128,1024]{2,1,0:T(8,128)(2,1)S(1)}, u32[]{:S(2)}, u32[]{:S(2)}) collective-permute-start(bf16[2,128,1024]{2,1,0:T(8,128)(2,1)} %get-tuple-element.51), channel_id=1, source_target_pairs={{0,48},{16,0},{32,16},{48,32},{1,49},{17,1},{33,17},{49,33},{2,50}... | collective-permute-start | bytes 1572872 | tf_op jit(solution)/shard_map/ppermute | solution.py:317
  10.4 14.4 %collective-permute-start.2 = (bf16[2,128,1024]{2,1,0:T(8,128)(2,1)}, bf16[2,128,1024]{2,1,0:T(8,128)(2,1)S(1)}, u32[]{:S(2)}, u32[]{:S(2)}) collective-permute-start(bf16[2,128,1024]{2,1,0:T(8,128)(2,1)} %get-tuple-element.48), channel_id=1, source_target_pairs={{0,16},{16,32},{32,48},{48,0},{1,17},{17,33},{33,49},{49,1},{2,18}... | collective-permute-start | bytes 1572872 | tf_op jit(solution)/shard_map/ppermute | solution.py:317
  10.4 14.6 %collective-permute-start.1 = (bf16[2,128,1024]{2,1,0:T(8,128)(2,1)}, bf16[2,128,1024]{2,1,0:T(8,128)(2,1)S(1)}, u32[]{:S(2)}, u32[]{:S(2)}) collective-permute-start(bf16[2,128,1024]{2,1,0:T(8,128)(2,1)} %get-tuple-element.45), channel_id=1, source_target_pairs={{0,192},{64,0},{128,64},{192,128},{1,193},{65,1},{129,65},{193,129... | collective-permute-start | bytes 1572872 | tf_op jit(solution)/shard_map/ppermute | solution.py:317
  13.3 14.8 %collective-permute-start = (bf16[2,128,1024]{2,1,0:T(8,128)(2,1)S(1)}, bf16[2,128,1024]{2,1,0:T(8,128)(2,1)S(1)}, u32[]{:S(2)}, u32[]{:S(2)}) collective-permute-start(bf16[2,128,1024]{2,1,0:T(8,128)(2,1)S(1)} %get-tuple-element.42), channel_id=1, source_target_pairs={{0,64},{64,128},{128,192},{192,0},{1,65},{65,129},{129,193},{193,1... | collective-permute-start | bytes 1572872 | tf_op jit(solution)/shard_map/ppermute | solution.py:317
  21.5 24.4 %collective-permute-start.18 = (bf16[4,128,1024]{2,1,0:T(8,128)(2,1)S(1)}, bf16[4,128,1024]{2,1,0:T(8,128)(2,1)S(1)}, u32[]{:S(2)}, u32[]{:S(2)}) collective-permute-start(bf16[4,128,1024]{2,1,0:T(8,128)(2,1)S(1)} %shard_map.83.rest_3_), channel_id=1, source_target_pairs={{0,48},{16,0},{32,16},{48,32},{1,49},{17,1},{33,17},{49,33},{2,50}... | collective-permute-start | bytes 3145736 | tf_op jit(solution)/shard_map/ppermute | solution.py:317
  24.9 24.2 %collective-permute-start.17 = (bf16[4,128,1024]{2,1,0:T(8,128)(2,1)S(1)}, bf16[4,128,1024]{2,1,0:T(8,128)(2,1)S(1)}, u32[]{:S(2)}, u32[]{:S(2)}) collective-permute-start(bf16[4,128,1024]{2,1,0:T(8,128)(2,1)S(1)} %shard_map.82.rest_2_), channel_id=1, source_target_pairs={{0,16},{16,32},{32,48},{48,0},{1,17},{17,33},{33,49},{49,1},{2,18}... | collective-permute-start | bytes 3145736 | tf_op jit(solution)/shard_map/ppermute | solution.py:317
  25.1 29.2 %collective-permute-start.5 = (bf16[4,128,1024]{2,1,0:T(8,128)(2,1)S(1)}, bf16[4,128,1024]{2,1,0:T(8,128)(2,1)S(1)}, u32[]{:S(2)}, u32[]{:S(2)}) collective-permute-start(bf16[4,128,1024]{2,1,0:T(8,128)(2,1)S(1)} %shard_map.81.rest_1_), channel_id=1, source_target_pairs={{0,192},{64,0},{128,64},{192,128},{1,193},{65,1},{129,65},{193,129... | collective-permute-start | bytes 3145736 | tf_op jit(solution)/shard_map/ppermute | solution.py:317
  28.2 26.2 %collective-permute-start.4 = (bf16[4,128,1024]{2,1,0:T(8,128)(2,1)S(1)}, bf16[4,128,1024]{2,1,0:T(8,128)(2,1)S(1)}, u32[]{:S(2)}, u32[]{:S(2)}) collective-permute-start(bf16[4,128,1024]{2,1,0:T(8,128)(2,1)S(1)} %shard_map.80.rest_0_), channel_id=1, source_target_pairs={{0,64},{64,128},{128,192},{192,0},{1,65},{65,129},{129,193},{193,1... | collective-permute-start | bytes 3145736 | tf_op jit(solution)/shard_map/ppermute | solution.py:317
  49.7 8.1 %copy-start.1 = (bf16[2,1,1,1024,1024]{4,3,2,1,0:T(8,128)(2,1)S(1)}, bf16[2,1,1,1024,1024]{4,3,2,1,0:T(8,128)(2,1)}, u32[]{:S(2)}) copy-start(bf16[2,1,1,1024,1024]{4,3,2,1,0:T(8,128)(2,1)} %param.11) | copy-start | bytes 12582916
  49.7 8.1 %copy-start.4 = (bf16[2,1,1,1024,128]{4,3,2,1,0:T(8,128)(2,1)S(1)}, bf16[2,1,1,1024,128]{4,3,2,1,0:T(8,128)(2,1)}, u32[]{:S(2)}) copy-start(bf16[2,1,1,1024,128]{4,3,2,1,0:T(8,128)(2,1)} %param.9) | copy-start | bytes 1572868
  49.8 9.2 %collective-permute-start.20 = (f16[144,1024]{1,0:T(8,128)(2,1)S(1)}, f16[144,1024]{1,0:T(8,128)(2,1)S(1)}, u32[]{:S(2)}, u32[]{:S(2)}) collective-permute-start(f16[144,1024]{1,0:T(8,128)(2,1)S(1)} %convert_element_type.30), channel_id=1, source_target_pairs={{0,64},{64,128},{128,192},{192,0},{1,65},{65,129},{129,193},{193,1... | collective-permute-start | bytes 884744 | tf_op jit(solution)/shard_map/ppermute | solution.py:317
  51.3 9.2 %collective-permute-start.21 = (f16[144,1024]{1,0:T(8,128)(2,1)S(1)}, f16[144,1024]{1,0:T(8,128)(2,1)S(1)}, u32[]{:S(2)}, u32[]{:S(2)}) collective-permute-start(f16[144,1024]{1,0:T(8,128)(2,1)S(1)} %convert_element_type.32), channel_id=1, source_target_pairs={{0,192},{64,0},{128,64},{192,128},{1,193},{65,1},{129,65},{193,129... | collective-permute-start | bytes 884744 | tf_op jit(solution)/shard_map/ppermute | solution.py:317
  52.9 10.8 %collective-permute-start.19 = (bf16[128,1024]{1,0:T(8,128)(2,1)S(1)}, bf16[128,1024]{1,0:T(8,128)(2,1)S(1)}, u32[]{:S(2)}, u32[]{:S(2)}) collective-permute-start(bf16[128,1024]{1,0:T(8,128)(2,1)S(1)} %get-tuple-element.66), channel_id=1, source_target_pairs={{0,128},{64,192},{128,0},{192,64},{1,129},{65,193},{129,1},{193,65... | collective-permute-start | bytes 786440 | tf_op jit(solution)/shard_map/ppermute | solution.py:317
  55.0 10.9 %collective-permute-start.7 = (f16[144,1024]{1,0:T(8,128)(2,1)S(1)}, f16[144,1024]{1,0:T(8,128)(2,1)S(1)}, u32[]{:S(2)}, u32[]{:S(2)}) collective-permute-start(f16[144,1024]{1,0:T(8,128)(2,1)S(1)} %convert_element_type.26), channel_id=1, source_target_pairs={{0,16},{16,32},{32,48},{48,0},{1,17},{17,33},{33,49},{49,1},{2,18}... | collective-permute-start | bytes 884744 | tf_op jit(solution)/shard_map/ppermute | solution.py:317
  55.1 12.3 %collective-permute-start.8 = (f16[144,1024]{1,0:T(8,128)(2,1)S(1)}, f16[144,1024]{1,0:T(8,128)(2,1)S(1)}, u32[]{:S(2)}, u32[]{:S(2)}) collective-permute-start(f16[144,1024]{1,0:T(8,128)(2,1)S(1)} %convert_element_type.28), channel_id=1, source_target_pairs={{0,48},{16,0},{32,16},{48,32},{1,49},{17,1},{33,17},{49,33},{2,50}... | collective-permute-start | bytes 884744 | tf_op jit(solution)/shard_map/ppermute | solution.py:317
  59.0 13.2 %collective-permute-start.6 = (bf16[128,1024]{1,0:T(8,128)(2,1)S(1)}, bf16[128,1024]{1,0:T(8,128)(2,1)S(1)}, u32[]{:S(2)}, u32[]{:S(2)}) collective-permute-start(bf16[128,1024]{1,0:T(8,128)(2,1)S(1)} %get-tuple-element.55), channel_id=1, source_target_pairs={{0,32},{16,48},{32,0},{48,16},{1,33},{17,49},{33,1},{49,17},{2,34}... | collective-permute-start | bytes 786440 | tf_op jit(solution)/shard_map/ppermute | solution.py:317
  64.6 12.4 %collective-permute-start.22 = (bf16[128,1024]{1,0:T(8,128)(2,1)S(1)}, bf16[128,1024]{1,0:T(8,128)(2,1)S(1)}, u32[]{:S(2)}, u32[]{:S(2)}) collective-permute-start(bf16[128,1024]{1,0:T(8,128)(2,1)S(1)} %get-tuple-element.71), channel_id=1, source_target_pairs={{0,16},{32,48},{64,80},{96,112},{128,144},{160,176},{192,208},{224... | collective-permute-start | bytes 786440 | tf_op jit(solution)/shard_map/ppermute | solution.py:322
  64.7 12.3 %collective-permute-start.23 = (bf16[128,1024]{1,0:T(8,128)(2,1)S(1)}, bf16[128,1024]{1,0:T(8,128)(2,1)S(1)}, u32[]{:S(2)}, u32[]{:S(2)}) collective-permute-start(bf16[128,1024]{1,0:T(8,128)(2,1)S(1)} %get-tuple-element.71), channel_id=1, source_target_pairs={{16,32},{48,64},{80,96},{112,128},{144,160},{176,192},{208,224},{2... | collective-permute-start | bytes 786440 | tf_op jit(solution)/shard_map/ppermute | solution.py:322
  65.9 15.1 %collective-permute-start.24 = (bf16[128,1024]{1,0:T(8,128)(2,1)S(1)}, bf16[128,1024]{1,0:T(8,128)(2,1)S(1)}, u32[]{:S(2)}, u32[]{:S(2)}) collective-permute-start(bf16[128,1024]{1,0:T(8,128)(2,1)S(1)} %get-tuple-element.71), channel_id=1, source_target_pairs={{0,2},{4,6},{8,10},{12,14},{2,0},{6,4},{10,8},{14,12},{1,3},{5,7},... | collective-permute-start | bytes 786440 | tf_op jit(solution)/shard_map/ppermute | solution.py:322
  67.5 13.5 %collective-permute-start.25 = (bf16[128,1024]{1,0:T(8,128)(2,1)S(1)}, bf16[128,1024]{1,0:T(8,128)(2,1)S(1)}, u32[]{:S(2)}, u32[]{:S(2)}) collective-permute-start(bf16[128,1024]{1,0:T(8,128)(2,1)S(1)} %get-tuple-element.71), channel_id=1, source_target_pairs={{2,4},{6,8},{10,12},{14,0},{4,2},{8,6},{12,10},{0,14},{3,5},{7,9},... | collective-permute-start | bytes 786440 | tf_op jit(solution)/shard_map/ppermute | solution.py:322
  72.1 8.8 %copy-start.3 = (f32[2,1,1,4,1024]{4,3,2,1,0:T(4,128)S(1)}, f32[2,1,1,4,1024]{4,3,2,1,0:T(4,128)}, u32[]{:S(2)}) copy-start(f32[2,1,1,4,1024]{4,3,2,1,0:T(4,128)} %param.10) | copy-start | bytes 98308
  73.1 10.8 %collective-permute-start.10 = (bf16[128,1024]{1,0:T(8,128)(2,1)S(1)}, bf16[128,1024]{1,0:T(8,128)(2,1)S(1)}, u32[]{:S(2)}, u32[]{:S(2)}) collective-permute-start(bf16[128,1024]{1,0:T(8,128)(2,1)S(1)} %get-tuple-element.61), channel_id=1, source_target_pairs={{16,32},{48,64},{80,96},{112,128},{144,160},{176,192},{208,224},{2... | collective-permute-start | bytes 786440 | tf_op jit(solution)/shard_map/ppermute | solution.py:322
  76.9 11.2 %collective-permute-start.11 = (bf16[128,1024]{1,0:T(8,128)(2,1)S(1)}, bf16[128,1024]{1,0:T(8,128)(2,1)S(1)}, u32[]{:S(2)}, u32[]{:S(2)}) collective-permute-start(bf16[128,1024]{1,0:T(8,128)(2,1)S(1)} %get-tuple-element.61), channel_id=1, source_target_pairs={{0,2},{4,6},{8,10},{12,14},{2,0},{6,4},{10,8},{14,12},{1,3},{5,7},... | collective-permute-start | bytes 786440 | tf_op jit(solution)/shard_map/ppermute | solution.py:322
  76.9 11.2 %collective-permute-start.12 = (bf16[128,1024]{1,0:T(8,128)(2,1)S(1)}, bf16[128,1024]{1,0:T(8,128)(2,1)S(1)}, u32[]{:S(2)}, u32[]{:S(2)}) collective-permute-start(bf16[128,1024]{1,0:T(8,128)(2,1)S(1)} %get-tuple-element.61), channel_id=1, source_target_pairs={{2,4},{6,8},{10,12},{14,0},{4,2},{8,6},{12,10},{0,14},{3,5},{7,9},... | collective-permute-start | bytes 786440 | tf_op jit(solution)/shard_map/ppermute | solution.py:322
  81.0 10.3 %collective-permute-start.9 = (bf16[128,1024]{1,0:T(8,128)(2,1)S(1)}, bf16[128,1024]{1,0:T(8,128)(2,1)S(1)}, u32[]{:S(2)}, u32[]{:S(2)}) collective-permute-start(bf16[128,1024]{1,0:T(8,128)(2,1)S(1)} %get-tuple-element.61), channel_id=1, source_target_pairs={{0,16},{32,48},{64,80},{96,112},{128,144},{160,176},{192,208},{224... | collective-permute-start | bytes 786440 | tf_op jit(solution)/shard_map/ppermute | solution.py:322
  82.4 10.4 %collective-permute-start.26 = (bf16[128,1024]{1,0:T(8,128)(2,1)S(1)}, bf16[128,1024]{1,0:T(8,128)(2,1)S(1)}, u32[]{:S(2)}, u32[]{:S(2)}) collective-permute-start(bf16[128,1024]{1,0:T(8,128)(2,1)S(1)} %get-tuple-element.73), channel_id=1, source_target_pairs={{0,16},{32,48},{64,80},{96,112},{128,144},{160,176},{192,208},{224... | collective-permute-start | bytes 786440 | tf_op jit(solution)/shard_map/ppermute | solution.py:322
  83.9 11.2 %collective-permute-start.27 = (bf16[128,1024]{1,0:T(8,128)(2,1)S(1)}, bf16[128,1024]{1,0:T(8,128)(2,1)S(1)}, u32[]{:S(2)}, u32[]{:S(2)}) collective-permute-start(bf16[128,1024]{1,0:T(8,128)(2,1)S(1)} %get-tuple-element.73), channel_id=1, source_target_pairs={{16,32},{48,64},{80,96},{112,128},{144,160},{176,192},{208,224},{2... | collective-permute-start | bytes 786440 | tf_op jit(solution)/shard_map/ppermute | solution.py:322
  88.1 7.0 %collective-permute-start.28 = (bf16[128,1024]{1,0:T(8,128)(2,1)S(1)}, bf16[128,1024]{1,0:T(8,128)(2,1)S(1)}, u32[]{:S(2)}, u32[]{:S(2)}) collective-permute-start(bf16[128,1024]{1,0:T(8,128)(2,1)S(1)} %get-tuple-element.73), channel_id=1, source_target_pairs={{0,2},{4,6},{8,10},{12,14},{2,0},{6,4},{10,8},{14,12},{1,3},{5,7},... | collective-permute-start | bytes 786440 | tf_op jit(solution)/shard_map/ppermute | solution.py:322
  88.1 7.9 %collective-permute-start.29 = (bf16[128,1024]{1,0:T(8,128)(2,1)S(1)}, bf16[128,1024]{1,0:T(8,128)(2,1)S(1)}, u32[]{:S(2)}, u32[]{:S(2)}) collective-permute-start(bf16[128,1024]{1,0:T(8,128)(2,1)S(1)} %get-tuple-element.73), channel_id=1, source_target_pairs={{2,4},{6,8},{10,12},{14,0},{4,2},{8,6},{12,10},{0,14},{3,5},{7,9},... | collective-permute-start | bytes 786440 | tf_op jit(solution)/shard_map/ppermute | solution.py:322
  92.7 6.5 %collective-permute-start.13 = (bf16[128,1024]{1,0:T(8,128)(2,1)S(1)}, bf16[128,1024]{1,0:T(8,128)(2,1)S(1)}, u32[]{:S(2)}, u32[]{:S(2)}) collective-permute-start(bf16[128,1024]{1,0:T(8,128)(2,1)S(1)} %get-tuple-element.63), channel_id=1, source_target_pairs={{0,16},{32,48},{64,80},{96,112},{128,144},{160,176},{192,208},{224... | collective-permute-start | bytes 786440 | tf_op jit(solution)/shard_map/ppermute | solution.py:322
  92.8 10.1 %collective-permute-start.14 = (bf16[128,1024]{1,0:T(8,128)(2,1)S(1)}, bf16[128,1024]{1,0:T(8,128)(2,1)S(1)}, u32[]{:S(2)}, u32[]{:S(2)}) collective-permute-start(bf16[128,1024]{1,0:T(8,128)(2,1)S(1)} %get-tuple-element.63), channel_id=1, source_target_pairs={{16,32},{48,64},{80,96},{112,128},{144,160},{176,192},{208,224},{2... | collective-permute-start | bytes 786440 | tf_op jit(solution)/shard_map/ppermute | solution.py:322
  95.1 8.0 %collective-permute-start.15 = (bf16[128,1024]{1,0:T(8,128)(2,1)S(1)}, bf16[128,1024]{1,0:T(8,128)(2,1)S(1)}, u32[]{:S(2)}, u32[]{:S(2)}) collective-permute-start(bf16[128,1024]{1,0:T(8,128)(2,1)S(1)} %get-tuple-element.63), channel_id=1, source_target_pairs={{0,2},{4,6},{8,10},{12,14},{2,0},{6,4},{10,8},{14,12},{1,3},{5,7},... | collective-permute-start | bytes 786440 | tf_op jit(solution)/shard_map/ppermute | solution.py:322
  95.2 9.1 %collective-permute-start.16 = (bf16[128,1024]{1,0:T(8,128)(2,1)S(1)}, bf16[128,1024]{1,0:T(8,128)(2,1)S(1)}, u32[]{:S(2)}, u32[]{:S(2)}) collective-permute-start(bf16[128,1024]{1,0:T(8,128)(2,1)S(1)} %get-tuple-element.63), channel_id=1, source_target_pairs={{2,4},{6,8},{10,12},{14,0},{4,2},{8,6},{12,10},{0,14},{3,5},{7,9},... | collective-permute-start | bytes 786440 | tf_op jit(solution)/shard_map/ppermute | solution.py:322

commit v2 on v1

--- a/solution.py
+++ b/solution.py
@@ -342,7 +342,9 @@
     axes = (SX, SX[::-1])
     plan = tuple((2 * f + n, 0, f, 2, pair) for f in range(2) for n, pair in enumerate((LOW, HIGH)))
     far = owner_products(plan, ((2, half),) * 4, *data, fetched=True)
-    got = [(turn(far[2 * f], axes[f][0], 1), turn(far[2 * f + 1], axes[f][0], -1)) for f in range(2)]
+    got = []
+    for f in range(2):
+        got.append((turn(far[2 * f], axes[f][0], 1), turn(far[2 * f + 1], axes[f][0], -1)))
 
     sides = ((1, LOW, HIGH), (3, HIGH, LOW))
     plan = tuple(
@@ -364,7 +366,7 @@
     rhs, matrix = staged(sep_rhs[:, 0, 0], frontal_inverse[:, 0, 0])
 
     coupling_rows = coupling[:, 0, 0]
-    order = (1, 0)
+    order = (0, 1)
     right_side, mine, sent = {}, {}, {}
     for f in order:
         here, following, preceding, opposite = row_totals(own[f], *sums[f])

time: 138 us -> 147 us (1.065)
  blocking collectives: 29.2 us -> 38.4 us
    all_to_all x1, blocking collectives: 19 us -> 27.5 us  [on_device(): squares = jnp.sum(lax.all_to_all(squares, group, 0, 0, tiled=True), axis=0)]
    ppermute x16, waiting for transfers between devices: 5.99 us -> 4.24 us  [neighbours(): lax.ppermute(x, axis, p + [(b, a) for a, b in p])]
    ppermute x16, starting transfers between devices: 27.5 us -> 29.1 us  [neighbours(): lax.ppermute(x, axis, p + [(b, a) for a, b in p])]
  transfers between devices with their start and end apart: 30 -> 30, of which waited for: 9 -> 7; matrix products, arithmetic and copies ran while one was open for 0% -> 0% of each run, Pallas kernels for 9% -> 9%
where the time goes in v2:
time: 147 us
  starting transfers between devices  49.8 us (34%)
  blocking collectives  38.4 us (26%)
  waiting for transfers between devices  33.5 us (23%)
  Pallas kernels  20.8 us (14%)
  between operations  2.8 us (2%)
    ppermute x14, waiting for transfers between devices, turn(): return lax.ppermute(x, axis, [(i, (i + by) % SIDE) for i in range(SIDE)])  29.3 us
    ppermute x16, starting transfers between devices, neighbours(): lax.ppermute(x, axis, p + [(b, a) for a, b in p])  29.1 us
    all_to_all x1, blocking collectives, on_device(): squares = jnp.sum(lax.all_to_all(squares, group, 0, 0, tiled=True), axis=0)  27.5 us
    ppermute x14, starting transfers between devices, turn(): return lax.ppermute(x, axis, [(i, (i + by) % SIDE) for i in range(SIDE)])  20.7 us
    all_to_all x1, blocking collectives, on_device(): squares = jnp.sum(lax.all_to_all(squares, SX, 0, 0, tiled=True), axis=0)  10.9 us
    pallas_call x3, Pallas kernels, owner_products(): pl.pallas_call(body, in_specs=[pl.BlockSpec(memory_space=pltpu.MemorySpac...  9.74 us
    pallas_call x2, Pallas kernels, last_sweep(): pl.pallas_call(body, grid=(1,), in_specs=[pl.BlockSpec(memory_space=pltpu...  4.49 us
    ppermute x16, waiting for transfers between devices, neighbours(): lax.ppermute(x, axis, p + [(b, a) for a, b in p])  4.24 us
  transfers between devices with their start and end apart: 30, of which 7 were waited for; matrix products, arithmetic and copies ran while one was open for 0% of the time, Pallas kernels for 9%

profile of v2, /device:TPU:1, one launch (start us, length us, event | category | flops | bytes accessed | tf_op | source)
XLA Modules:
  0.0 147.0 jit_solution(1166009311082208524)
XLA Ops:
  0.7 0.1 stack.51.table_ref
  0.8 0.8 copy-done.5
  1.6 5.5 %shard_map.79 = (bf16[2,128,1024]{2,1,0:T(8,128)(2,1)S(1)}, bf16[2,128,1024]{2,1,0:T(8,128)(2,1)}, bf16[2,128,1024]{2,1,0:T(8,128)(2,1)}, bf16[2,128,1024]{2,1,0:T(8,128)(2,1)}) custom-call(s32[32]{0:T(128)S(1)} %bitcast.24, s32[12]{0:T(128)S(1)} %stack.51.table_ref, bf16[2,32,32,1024]{3,2,1,0:T(8,128)(2,1)} %basis_ref.5, bf16[2,32,32,128]{3,2,1,0:T(8,128)(2,1)} %coeff_ref.5), custom_call_target="tpu_custom_call" | custom-call | flops 1073741824 | bytes 6291456 | tf_op jit(solution)/shard_map/pallas_call | solution.py:119
  7.1 3.8 %collective-permute-start.1 = (bf16[2,128,1024]{2,1,0:T(8,128)(2,1)}, bf16[2,128,1024]{2,1,0:T(8,128)(2,1)S(1)}, u32[]{:S(2)}, u32[]{:S(2)}) collective-permute-start(bf16[2,128,1024]{2,1,0:T(8,128)(2,1)} %get-tuple-element.45), channel_id=1, source_target_pairs={{0,192},{64,0},{128,64},{192,128},{1,193},{65,1},{129,65},{193,129... | collective-permute-start | bytes 1572872 | tf_op jit(solution)/shard_map/ppermute | solution.py:317
  10.9 2.5 %collective-permute-start.3 = (bf16[2,128,1024]{2,1,0:T(8,128)(2,1)}, bf16[2,128,1024]{2,1,0:T(8,128)(2,1)S(1)}, u32[]{:S(2)}, u32[]{:S(2)}) collective-permute-start(bf16[2,128,1024]{2,1,0:T(8,128)(2,1)} %get-tuple-element.51), channel_id=1, source_target_pairs={{0,48},{16,0},{32,16},{48,32},{1,49},{17,1},{33,17},{49,33},{2,50}... | collective-permute-start | bytes 1572872 | tf_op jit(solution)/shard_map/ppermute | solution.py:317
  13.3 2.4 %shard_map.78 = (f32[2,128,1024]{2,1,0:T(8,128)S(1)}, f32[2,128,1024]{2,1,0:T(8,128)S(1)}, f32[2,128,1024]{2,1,0:T(8,128)S(1)}, f32[2,128,1024]{2,1,0:T(8,128)S(...) custom-call(s32[32]{0:T(128)S(1)} %bitcast.25, ...), custom_call_target="tpu_custom_call" | custom-call | flops 2147483648 | bytes 12582912 | tf_op jit(solution)/shard_map/pallas_call | solution.py:119
  15.7 6.0 %collective-permute-done.1.got_ref = bf16[2,128,1024]{2,1,0:T(8,128)(2,1)S(1)} collective-permute-done((bf16[2,128,1024]{2,1,0:T(8,128)(2,1)}, bf16[2,128,1024]{2,1,0:T(8,128)(2,1)S(1)}, u32[]{:S(2)}, u32[]{:S(2)}) %collective-permute-start.1) | collective-permute-done | bytes 524320 | tf_op jit(solution)/shard_map/ppermute | solution.py:317
  21.8 0.1 shard_map.81.rest_1_
  21.9 3.4 %collective-permute-start.18 = (bf16[4,128,1024]{2,1,0:T(8,128)(2,1)S(1)}, bf16[4,128,1024]{2,1,0:T(8,128)(2,1)S(1)}, u32[]{:S(2)}, u32[]{:S(2)}) collective-permute-start(bf16[4,128,1024]{2,1,0:T(8,128)(2,1)S(1)} %shard_map.81.rest_1_), channel_id=1, source_target_pairs={{0,192},{64,0},{128,64},{192,128},{1,193},{65,1},{129,65},{193,129... | collective-permute-start | bytes 3145736 | tf_op jit(solution)/shard_map/ppermute | solution.py:317
  25.5 0.1 shard_map.83.rest_3_
  25.5 2.5 %collective-permute-start.5 = (bf16[4,128,1024]{2,1,0:T(8,128)(2,1)S(1)}, bf16[4,128,1024]{2,1,0:T(8,128)(2,1)S(1)}, u32[]{:S(2)}, u32[]{:S(2)}) collective-permute-start(bf16[4,128,1024]{2,1,0:T(8,128)(2,1)S(1)} %shard_map.83.rest_3_), channel_id=1, source_target_pairs={{0,48},{16,0},{32,16},{48,32},{1,49},{17,1},{33,17},{49,33},{2,50}... | collective-permute-start | bytes 3145736 | tf_op jit(solution)/shard_map/ppermute | solution.py:317
  28.3 1.8 %shard_map.84 = (f32[4,128,1024]{2,1,0:T(8,128)S(1)}, f32[4,128,1024]{2,1,0:T(8,128)S(1)}) custom-call(s32[32]{0:T(128)S(1)} %bitcast.26, s32[12]{0:T(128)S(1)} %stack.51.table_ref, bf16[2,32,32,1024]{3,2,1,0:T(8,128)(2,1)S(1)} %copy-done, bf16[2,32,32,128]{3,2,1,0:T(8,128)(2,1)S(1)} %copy-done.2, bf16[4,128,1024]{2,1,0:T(8,128)(2,1)S(1)} %shard_map.80.rest_0_, ...), custom_call_target="tpu_custom_call" | custom-call | flops 1073741824 | bytes 6291456 | tf_op jit(solution)/shard_map/pallas_call | solution.py:119
  30.1 16.1 %collective-permute-done.18.high_ref = bf16[4,128,1024]{2,1,0:T(8,128)(2,1)S(1)} collective-permute-done((bf16[4,128,1024]{2,1,0:T(8,128)(2,1)S(1)}, bf16[4,128,1024]{2,1,0:T(8,128)(2,1)S(1)}, u32[]{:S(2)}, u32[]{:S(2)}) %collective-permute-start.18) | collective-permute-done | bytes 1048608 | tf_op jit(solution)/shard_map/ppermute | solution.py:317
  46.2 3.3 %collective-permute-done.17.low_ref = bf16[4,128,1024]{2,1,0:T(8,128)(2,1)S(1)} collective-permute-done((bf16[4,128,1024]{2,1,0:T(8,128)(2,1)S(1)}, bf16[4,128,1024]{2,1,0:T(8,128)(2,1)S(1)}, u32[]{:S(2)}, u32[]{:S(2)}) %collective-permute-start.17) | collective-permute-done | bytes 1048608 | tf_op jit(solution)/shard_map/ppermute | solution.py:317
  49.5 0.6 shard_map.88
  50.2 1.2 collective-permute-start.20
  51.5 1.6 %collective-permute-start.21 = (f16[144,1024]{1,0:T(8,128)(2,1)S(1)}, f16[144,1024]{1,0:T(8,128)(2,1)S(1)}, u32[]{:S(2)}, u32[]{:S(2)}) collective-permute-start(f16[144,1024]{1,0:T(8,128)(2,1)S(1)} %convert_element_type.32), channel_id=1, source_target_pairs={{0,48},{16,0},{32,16},{48,32},{1,49},{17,1},{33,17},{49,33},{2,50}... | collective-permute-start | bytes 884744 | tf_op jit(solution)/shard_map/ppermute | solution.py:317
  53.1 1.5 collective-permute-start.19
  54.6 0.6 shard_map.85
  55.3 2.7 %collective-permute-start.8 = (f16[144,1024]{1,0:T(8,128)(2,1)S(1)}, f16[144,1024]{1,0:T(8,128)(2,1)S(1)}, u32[]{:S(2)}, u32[]{:S(2)}) collective-permute-start(f16[144,1024]{1,0:T(8,128)(2,1)S(1)} %convert_element_type.28), channel_id=1, source_target_pairs={{0,192},{64,0},{128,64},{192,128},{1,193},{65,1},{129,65},{193,129... | collective-permute-start | bytes 884744 | tf_op jit(solution)/shard_map/ppermute | solution.py:317
  58.1 0.4 shard_map.77
  58.5 1.3 collective-permute-start.6
  59.9 3.7 %collective-permute-done.19.rest_1_ = bf16[128,1024]{1,0:T(8,128)(2,1)S(1)} collective-permute-done((bf16[128,1024]{1,0:T(8,128)(2,1)S(1)}, bf16[128,1024]{1,0:T(8,128)(2,1)S(1)}, u32[]{:S(2)}, u32[]{:S(2)}) %collective-permute-start.19) | collective-permute-done | bytes 262176 | tf_op jit(solution)/shard_map/ppermute | solution.py:317
  63.7 0.9 shard_map.89
  64.6 1.1 collective-permute-start.22
  65.7 3.0 %collective-permute-start.23 = (bf16[128,1024]{1,0:T(8,128)(2,1)S(1)}, bf16[128,1024]{1,0:T(8,128)(2,1)S(1)}, u32[]{:S(2)}, u32[]{:S(2)}) collective-permute-start(bf16[128,1024]{1,0:T(8,128)(2,1)S(1)} %get-tuple-element.71), channel_id=1, source_target_pairs={{16,32},{48,64},{80,96},{112,128},{144,160},{176,192},{208,224},{2... | collective-permute-start | bytes 786440 | tf_op jit(solution)/shard_map/ppermute | solution.py:322
  68.7 1.7 %collective-permute-start.24 = (bf16[128,1024]{1,0:T(8,128)(2,1)S(1)}, bf16[128,1024]{1,0:T(8,128)(2,1)S(1)}, u32[]{:S(2)}, u32[]{:S(2)}) collective-permute-start(bf16[128,1024]{1,0:T(8,128)(2,1)S(1)} %get-tuple-element.71), channel_id=1, source_target_pairs={{0,2},{4,6},{8,10},{12,14},{2,0},{6,4},{10,8},{14,12},{1,3},{5,7},... | collective-permute-start | bytes 786440 | tf_op jit(solution)/shard_map/ppermute | solution.py:322
  70.4 4.7 %collective-permute-start.25 = (bf16[128,1024]{1,0:T(8,128)(2,1)S(1)}, bf16[128,1024]{1,0:T(8,128)(2,1)S(1)}, u32[]{:S(2)}, u32[]{:S(2)}) collective-permute-start(bf16[128,1024]{1,0:T(8,128)(2,1)S(1)} %get-tuple-element.71), channel_id=1, source_target_pairs={{2,4},{6,8},{10,12},{14,0},{4,2},{8,6},{12,10},{0,14},{3,5},{7,9},... | collective-permute-start | bytes 786440 | tf_op jit(solution)/shard_map/ppermute | solution.py:322
  75.2 0.9 shard_map.86
  76.1 1.7 %collective-permute-start.10 = (bf16[128,1024]{1,0:T(8,128)(2,1)S(1)}, bf16[128,1024]{1,0:T(8,128)(2,1)S(1)}, u32[]{:S(2)}, u32[]{:S(2)}) collective-permute-start(bf16[128,1024]{1,0:T(8,128)(2,1)S(1)} %get-tuple-element.61), channel_id=1, source_target_pairs={{16,32},{48,64},{80,96},{112,128},{144,160},{176,192},{208,224},{2... | collective-permute-start | bytes 786440 | tf_op jit(solution)/shard_map/ppermute | solution.py:322
  77.8 2.6 %collective-permute-start.12 = (bf16[128,1024]{1,0:T(8,128)(2,1)S(1)}, bf16[128,1024]{1,0:T(8,128)(2,1)S(1)}, u32[]{:S(2)}, u32[]{:S(2)}) collective-permute-start(bf16[128,1024]{1,0:T(8,128)(2,1)S(1)} %get-tuple-element.61), channel_id=1, source_target_pairs={{2,4},{6,8},{10,12},{14,0},{4,2},{8,6},{12,10},{0,14},{3,5},{7,9},... | collective-permute-start | bytes 786440 | tf_op jit(solution)/shard_map/ppermute | solution.py:322
  80.5 1.4 shard_map.90
  81.9 1.5 %collective-permute-start.26 = (bf16[128,1024]{1,0:T(8,128)(2,1)S(1)}, bf16[128,1024]{1,0:T(8,128)(2,1)S(1)}, u32[]{:S(2)}, u32[]{:S(2)}) collective-permute-start(bf16[128,1024]{1,0:T(8,128)(2,1)S(1)} %get-tuple-element.73), channel_id=1, source_target_pairs={{0,16},{32,48},{64,80},{96,112},{128,144},{160,176},{192,208},{224... | collective-permute-start | bytes 786440 | tf_op jit(solution)/shard_map/ppermute | solution.py:322
  83.5 1.3 collective-permute-done.10.rest_1_
  84.7 2.3 %collective-permute-start.27 = (bf16[128,1024]{1,0:T(8,128)(2,1)S(1)}, bf16[128,1024]{1,0:T(8,128)(2,1)S(1)}, u32[]{:S(2)}, u32[]{:S(2)}) collective-permute-start(bf16[128,1024]{1,0:T(8,128)(2,1)S(1)} %get-tuple-element.73), channel_id=1, source_target_pairs={{16,32},{48,64},{80,96},{112,128},{144,160},{176,192},{208,224},{2... | collective-permute-start | bytes 786440 | tf_op jit(solution)/shard_map/ppermute | solution.py:322
  87.1 0.2 collective-permute-start.28
  87.2 4.5 %collective-permute-start.29 = (bf16[128,1024]{1,0:T(8,128)(2,1)S(1)}, bf16[128,1024]{1,0:T(8,128)(2,1)S(1)}, u32[]{:S(2)}, u32[]{:S(2)}) collective-permute-start(bf16[128,1024]{1,0:T(8,128)(2,1)S(1)} %get-tuple-element.73), channel_id=1, source_target_pairs={{2,4},{6,8},{10,12},{14,0},{4,2},{8,6},{12,10},{0,14},{3,5},{7,9},... | collective-permute-start | bytes 786440 | tf_op jit(solution)/shard_map/ppermute | solution.py:322
  91.7 1.4 shard_map.87
  93.1 0.1 collective-permute-start.13
  93.2 1.3 collective-permute-start.14
  94.6 4.3 %collective-permute-start.16 = (bf16[128,1024]{1,0:T(8,128)(2,1)S(1)}, bf16[128,1024]{1,0:T(8,128)(2,1)S(1)}, u32[]{:S(2)}, u32[]{:S(2)}) collective-permute-start(bf16[128,1024]{1,0:T(8,128)(2,1)S(1)} %get-tuple-element.63), channel_id=1, source_target_pairs={{2,4},{6,8},{10,12},{14,0},{4,2},{8,6},{12,10},{0,14},{3,5},{7,9},... | collective-permute-start | bytes 786440 | tf_op jit(solution)/shard_map/ppermute | solution.py:322
  98.9 2.3 %shard_map.91 = (f32[2,1024,128]{2,1,0:T(8,128)}, f32[16,8,128]{2,1,0:T(8,128)S(1)}) custom-call(s32[12]{0:T(128)S(1)} %stack.51.table_ref, f32[128,1024]{1,0:T(8,128)S(1)} %get-tuple-element.69.right_ref, f32[128,1024]{1,0:T(8,128)S(1)} %get-tuple-element.72.mine_ref, bf16[128,1024]{1,0:T(8,128)(2,1)S(1)} %collective-permute-done.26.rest_0_, ...), custom_call_target="tpu_custom_call" | custom-call | flops 268435456 | bytes 5242880 | tf_op jit(solution)/shard_map/pallas_call | solution.py:299
  101.1 0.8 collective-permute-done.14.rest_1_
  101.9 2.2 %collective-permute-done.16.rest_3_ = bf16[128,1024]{1,0:T(8,128)(2,1)S(1)} collective-permute-done((bf16[128,1024]{1,0:T(8,128)(2,1)S(1)}, bf16[128,1024]{1,0:T(8,128)(2,1)S(1)}, u32[]{:S(2)}, u32[]{:S(2)}) %collective-permute-start.16) | collective-permute-done | bytes 262176 | tf_op jit(solution)/shard_map/ppermute | solution.py:322
  104.0 2.2 %shard_map.92 = (f32[2,1024,128]{2,1,0:T(8,128)}, f32[16,8,128]{2,1,0:T(8,128)S(1)}) custom-call(s32[12]{0:T(128)S(1)} %stack.51.table_ref, f32[128,1024]{1,0:T(8,128)S(1)} %get-tuple-element.59.right_ref, f32[128,1024]{1,0:T(8,128)S(1)} %get-tuple-element.62.mine_ref, ...), custom_call_target="tpu_custom_call", output_to_operand_aliasing={{0}: (9, {})} | custom-call | flops 268435456 | bytes 5242880 | tf_op jit(solution)/shard_map/pallas_call | solution.py:299
  106.3 27.5 %all_to_all.10 = f32[16,8,128]{2,1,0:T(8,128)S(1)} all-to-all(f32[16,8,128]{2,1,0:T(8,128)S(1)} %get-tuple-element.77), channel_id=1, replica_groups=mesh['sx_0'=4,'sx_1'=4,'sy'=8,'freq'=2] {'sy','freq'}, dimensions={0} | all-to-all | bytes 131072 | tf_op jit(solution)/shard_map/all_to_all | solution.py:393
  133.8 10.9 %all_to_all.11 = f32[16,8,128]{2,1,0:T(8,128)S(1)} all-to-all(f32[16,8,128]{2,1,0:T(8,128)S(1)} %broadcast_in_dim.7), channel_id=1, replica_groups=mesh['sx_0'=4,'sx_1'=4,'sy'=8,'freq'=2] {'sx_0','sx_1'}, dimensions={0} | all-to-all | bytes 131072 | tf_op jit(solution)/shard_map/all_to_all | solution.py:395
  144.7 0.5 slice.3
  (55 shorter events, 0.9 us)
Async XLA Ops:
  0.6 12.7 %copy-start.2 = (bf16[2,32,32,128]{3,2,1,0:T(8,128)(2,1)S(1)}, bf16[2,32,32,128]{3,2,1,0:T(8,128)(2,1)}, u32[]{:S(2)}) copy-start(bf16[2,32,32,128]{3,2,1,0:T(8,128)(2,1)} %coeff_ref.5) | copy-start | bytes 1572868
  0.8 12.6 %copy-start = (bf16[2,32,32,1024]{3,2,1,0:T(8,128)(2,1)S(1)}, bf16[2,32,32,1024]{3,2,1,0:T(8,128)(2,1)}, u32[]{:S(2)}) copy-start(bf16[2,32,32,1024]{3,2,1,0:T(8,128)(2,1)} %basis_ref.5) | copy-start | bytes 12582916
  0.8 0.8 copy-start.5
  7.1 14.7 %collective-permute-start.1 = (bf16[2,128,1024]{2,1,0:T(8,128)(2,1)}, bf16[2,128,1024]{2,1,0:T(8,128)(2,1)S(1)}, u32[]{:S(2)}, u32[]{:S(2)}) collective-permute-start(bf16[2,128,1024]{2,1,0:T(8,128)(2,1)} %get-tuple-element.45), channel_id=1, source_target_pairs={{0,192},{64,0},{128,64},{192,128},{1,193},{65,1},{129,65},{193,129... | collective-permute-start | bytes 1572872 | tf_op jit(solution)/shard_map/ppermute | solution.py:317
  10.9 14.4 %collective-permute-start = (bf16[2,128,1024]{2,1,0:T(8,128)(2,1)S(1)}, bf16[2,128,1024]{2,1,0:T(8,128)(2,1)S(1)}, u32[]{:S(2)}, u32[]{:S(2)}) collective-permute-start(bf16[2,128,1024]{2,1,0:T(8,128)(2,1)S(1)} %get-tuple-element.42), channel_id=1, source_target_pairs={{0,64},{64,128},{128,192},{192,0},{1,65},{65,129},{129,193},{193,1... | collective-permute-start | bytes 1572872 | tf_op jit(solution)/shard_map/ppermute | solution.py:317
  10.9 14.6 %collective-permute-start.3 = (bf16[2,128,1024]{2,1,0:T(8,128)(2,1)}, bf16[2,128,1024]{2,1,0:T(8,128)(2,1)S(1)}, u32[]{:S(2)}, u32[]{:S(2)}) collective-permute-start(bf16[2,128,1024]{2,1,0:T(8,128)(2,1)} %get-tuple-element.51), channel_id=1, source_target_pairs={{0,48},{16,0},{32,16},{48,32},{1,49},{17,1},{33,17},{49,33},{2,50}... | collective-permute-start | bytes 1572872 | tf_op jit(solution)/shard_map/ppermute | solution.py:317
  13.3 14.8 %collective-permute-start.2 = (bf16[2,128,1024]{2,1,0:T(8,128)(2,1)}, bf16[2,128,1024]{2,1,0:T(8,128)(2,1)S(1)}, u32[]{:S(2)}, u32[]{:S(2)}) collective-permute-start(bf16[2,128,1024]{2,1,0:T(8,128)(2,1)} %get-tuple-element.48), channel_id=1, source_target_pairs={{0,16},{16,32},{32,48},{48,0},{1,17},{17,33},{33,49},{49,1},{2,18}... | collective-permute-start | bytes 1572872 | tf_op jit(solution)/shard_map/ppermute | solution.py:317
  21.9 24.4 %collective-permute-start.18 = (bf16[4,128,1024]{2,1,0:T(8,128)(2,1)S(1)}, bf16[4,128,1024]{2,1,0:T(8,128)(2,1)S(1)}, u32[]{:S(2)}, u32[]{:S(2)}) collective-permute-start(bf16[4,128,1024]{2,1,0:T(8,128)(2,1)S(1)} %shard_map.81.rest_1_), channel_id=1, source_target_pairs={{0,192},{64,0},{128,64},{192,128},{1,193},{65,1},{129,65},{193,129... | collective-permute-start | bytes 3145736 | tf_op jit(solution)/shard_map/ppermute | solution.py:317
  25.3 24.2 %collective-permute-start.17 = (bf16[4,128,1024]{2,1,0:T(8,128)(2,1)S(1)}, bf16[4,128,1024]{2,1,0:T(8,128)(2,1)S(1)}, u32[]{:S(2)}, u32[]{:S(2)}) collective-permute-start(bf16[4,128,1024]{2,1,0:T(8,128)(2,1)S(1)} %shard_map.80.rest_0_), channel_id=1, source_target_pairs={{0,64},{64,128},{128,192},{192,0},{1,65},{65,129},{129,193},{193,1... | collective-permute-start | bytes 3145736 | tf_op jit(solution)/shard_map/ppermute | solution.py:317
  25.5 29.0 %collective-permute-start.5 = (bf16[4,128,1024]{2,1,0:T(8,128)(2,1)S(1)}, bf16[4,128,1024]{2,1,0:T(8,128)(2,1)S(1)}, u32[]{:S(2)}, u32[]{:S(2)}) collective-permute-start(bf16[4,128,1024]{2,1,0:T(8,128)(2,1)S(1)} %shard_map.83.rest_3_), channel_id=1, source_target_pairs={{0,48},{16,0},{32,16},{48,32},{1,49},{17,1},{33,17},{49,33},{2,50}... | collective-permute-start | bytes 3145736 | tf_op jit(solution)/shard_map/ppermute | solution.py:317
  28.2 26.4 %collective-permute-start.4 = (bf16[4,128,1024]{2,1,0:T(8,128)(2,1)S(1)}, bf16[4,128,1024]{2,1,0:T(8,128)(2,1)S(1)}, u32[]{:S(2)}, u32[]{:S(2)}) collective-permute-start(bf16[4,128,1024]{2,1,0:T(8,128)(2,1)S(1)} %shard_map.82.rest_2_), channel_id=1, source_target_pairs={{0,16},{16,32},{32,48},{48,0},{1,17},{17,33},{33,49},{49,1},{2,18}... | collective-permute-start | bytes 3145736 | tf_op jit(solution)/shard_map/ppermute | solution.py:317
  50.1 7.9 %copy-start.1 = (bf16[2,1,1,1024,1024]{4,3,2,1,0:T(8,128)(2,1)S(1)}, bf16[2,1,1,1024,1024]{4,3,2,1,0:T(8,128)(2,1)}, u32[]{:S(2)}) copy-start(bf16[2,1,1,1024,1024]{4,3,2,1,0:T(8,128)(2,1)} %param.11) | copy-start | bytes 12582916
  50.2 7.9 %copy-start.4 = (bf16[2,1,1,1024,128]{4,3,2,1,0:T(8,128)(2,1)S(1)}, bf16[2,1,1,1024,128]{4,3,2,1,0:T(8,128)(2,1)}, u32[]{:S(2)}) copy-start(bf16[2,1,1,1024,128]{4,3,2,1,0:T(8,128)(2,1)} %param.9) | copy-start | bytes 1572868
  50.2 8.3 %collective-permute-start.20 = (f16[144,1024]{1,0:T(8,128)(2,1)S(1)}, f16[144,1024]{1,0:T(8,128)(2,1)S(1)}, u32[]{:S(2)}, u32[]{:S(2)}) collective-permute-start(f16[144,1024]{1,0:T(8,128)(2,1)S(1)} %convert_element_type.30), channel_id=1, source_target_pairs={{0,16},{16,32},{32,48},{48,0},{1,17},{17,33},{33,49},{49,1},{2,18}... | collective-permute-start | bytes 884744 | tf_op jit(solution)/shard_map/ppermute | solution.py:317
  51.5 8.4 %collective-permute-start.21 = (f16[144,1024]{1,0:T(8,128)(2,1)S(1)}, f16[144,1024]{1,0:T(8,128)(2,1)S(1)}, u32[]{:S(2)}, u32[]{:S(2)}) collective-permute-start(f16[144,1024]{1,0:T(8,128)(2,1)S(1)} %convert_element_type.32), channel_id=1, source_target_pairs={{0,48},{16,0},{32,16},{48,32},{1,49},{17,1},{33,17},{49,33},{2,50}... | collective-permute-start | bytes 884744 | tf_op jit(solution)/shard_map/ppermute | solution.py:317
  53.1 10.6 %collective-permute-start.19 = (bf16[128,1024]{1,0:T(8,128)(2,1)S(1)}, bf16[128,1024]{1,0:T(8,128)(2,1)S(1)}, u32[]{:S(2)}, u32[]{:S(2)}) collective-permute-start(bf16[128,1024]{1,0:T(8,128)(2,1)S(1)} %get-tuple-element.66), channel_id=1, source_target_pairs={{0,32},{16,48},{32,0},{48,16},{1,33},{17,49},{33,1},{49,17},{2,34}... | collective-permute-start | bytes 786440 | tf_op jit(solution)/shard_map/ppermute | solution.py:317
  55.2 13.5 %collective-permute-start.7 = (f16[144,1024]{1,0:T(8,128)(2,1)S(1)}, f16[144,1024]{1,0:T(8,128)(2,1)S(1)}, u32[]{:S(2)}, u32[]{:S(2)}) collective-permute-start(f16[144,1024]{1,0:T(8,128)(2,1)S(1)} %convert_element_type.26), channel_id=1, source_target_pairs={{0,64},{64,128},{128,192},{192,0},{1,65},{65,129},{129,193},{193,1... | collective-permute-start | bytes 884744 | tf_op jit(solution)/shard_map/ppermute | solution.py:317
  55.3 15.0 %collective-permute-start.8 = (f16[144,1024]{1,0:T(8,128)(2,1)S(1)}, f16[144,1024]{1,0:T(8,128)(2,1)S(1)}, u32[]{:S(2)}, u32[]{:S(2)}) collective-permute-start(f16[144,1024]{1,0:T(8,128)(2,1)S(1)} %convert_element_type.28), channel_id=1, source_target_pairs={{0,192},{64,0},{128,64},{192,128},{1,193},{65,1},{129,65},{193,129... | collective-permute-start | bytes 884744 | tf_op jit(solution)/shard_map/ppermute | solution.py:317
  58.5 16.7 %collective-permute-start.6 = (bf16[128,1024]{1,0:T(8,128)(2,1)S(1)}, bf16[128,1024]{1,0:T(8,128)(2,1)S(1)}, u32[]{:S(2)}, u32[]{:S(2)}) collective-permute-start(bf16[128,1024]{1,0:T(8,128)(2,1)S(1)} %get-tuple-element.55), channel_id=1, source_target_pairs={{0,128},{64,192},{128,0},{192,64},{1,129},{65,193},{129,1},{193,65... | collective-permute-start | bytes 786440 | tf_op jit(solution)/shard_map/ppermute | solution.py:317
  64.6 13.3 %collective-permute-start.22 = (bf16[128,1024]{1,0:T(8,128)(2,1)S(1)}, bf16[128,1024]{1,0:T(8,128)(2,1)S(1)}, u32[]{:S(2)}, u32[]{:S(2)}) collective-permute-start(bf16[128,1024]{1,0:T(8,128)(2,1)S(1)} %get-tuple-element.71), channel_id=1, source_target_pairs={{0,16},{32,48},{64,80},{96,112},{128,144},{160,176},{192,208},{224... | collective-permute-start | bytes 786440 | tf_op jit(solution)/shard_map/ppermute | solution.py:322
  65.7 12.2 %collective-permute-start.23 = (bf16[128,1024]{1,0:T(8,128)(2,1)S(1)}, bf16[128,1024]{1,0:T(8,128)(2,1)S(1)}, u32[]{:S(2)}, u32[]{:S(2)}) collective-permute-start(bf16[128,1024]{1,0:T(8,128)(2,1)S(1)} %get-tuple-element.71), channel_id=1, source_target_pairs={{16,32},{48,64},{80,96},{112,128},{144,160},{176,192},{208,224},{2... | collective-permute-start | bytes 786440 | tf_op jit(solution)/shard_map/ppermute | solution.py:322
  68.7 11.8 %collective-permute-start.24 = (bf16[128,1024]{1,0:T(8,128)(2,1)S(1)}, bf16[128,1024]{1,0:T(8,128)(2,1)S(1)}, u32[]{:S(2)}, u32[]{:S(2)}) collective-permute-start(bf16[128,1024]{1,0:T(8,128)(2,1)S(1)} %get-tuple-element.71), channel_id=1, source_target_pairs={{0,2},{4,6},{8,10},{12,14},{2,0},{6,4},{10,8},{14,12},{1,3},{5,7},... | collective-permute-start | bytes 786440 | tf_op jit(solution)/shard_map/ppermute | solution.py:322
  70.4 10.1 %collective-permute-start.25 = (bf16[128,1024]{1,0:T(8,128)(2,1)S(1)}, bf16[128,1024]{1,0:T(8,128)(2,1)S(1)}, u32[]{:S(2)}, u32[]{:S(2)}) collective-permute-start(bf16[128,1024]{1,0:T(8,128)(2,1)S(1)} %get-tuple-element.71), channel_id=1, source_target_pairs={{2,4},{6,8},{10,12},{14,0},{4,2},{8,6},{12,10},{0,14},{3,5},{7,9},... | collective-permute-start | bytes 786440 | tf_op jit(solution)/shard_map/ppermute | solution.py:322
  75.1 5.4 %copy-start.3 = (f32[2,1,1,4,1024]{4,3,2,1,0:T(4,128)S(1)}, f32[2,1,1,4,1024]{4,3,2,1,0:T(4,128)}, u32[]{:S(2)}) copy-start(f32[2,1,1,4,1024]{4,3,2,1,0:T(4,128)} %param.10) | copy-start | bytes 98308
  76.1 8.6 %collective-permute-start.10 = (bf16[128,1024]{1,0:T(8,128)(2,1)S(1)}, bf16[128,1024]{1,0:T(8,128)(2,1)S(1)}, u32[]{:S(2)}, u32[]{:S(2)}) collective-permute-start(bf16[128,1024]{1,0:T(8,128)(2,1)S(1)} %get-tuple-element.61), channel_id=1, source_target_pairs={{16,32},{48,64},{80,96},{112,128},{144,160},{176,192},{208,224},{2... | collective-permute-start | bytes 786440 | tf_op jit(solution)/shard_map/ppermute | solution.py:322
  77.8 9.2 %collective-permute-start.11 = (bf16[128,1024]{1,0:T(8,128)(2,1)S(1)}, bf16[128,1024]{1,0:T(8,128)(2,1)S(1)}, u32[]{:S(2)}, u32[]{:S(2)}) collective-permute-start(bf16[128,1024]{1,0:T(8,128)(2,1)S(1)} %get-tuple-element.61), channel_id=1, source_target_pairs={{0,2},{4,6},{8,10},{12,14},{2,0},{6,4},{10,8},{14,12},{1,3},{5,7},... | collective-permute-start | bytes 786440 | tf_op jit(solution)/shard_map/ppermute | solution.py:322
  77.8 9.4 %collective-permute-start.12 = (bf16[128,1024]{1,0:T(8,128)(2,1)S(1)}, bf16[128,1024]{1,0:T(8,128)(2,1)S(1)}, u32[]{:S(2)}, u32[]{:S(2)}) collective-permute-start(bf16[128,1024]{1,0:T(8,128)(2,1)S(1)} %get-tuple-element.61), channel_id=1, source_target_pairs={{2,4},{6,8},{10,12},{14,0},{4,2},{8,6},{12,10},{0,14},{3,5},{7,9},... | collective-permute-start | bytes 786440 | tf_op jit(solution)/shard_map/ppermute | solution.py:322
  80.5 11.2 %collective-permute-start.9 = (bf16[128,1024]{1,0:T(8,128)(2,1)S(1)}, bf16[128,1024]{1,0:T(8,128)(2,1)S(1)}, u32[]{:S(2)}, u32[]{:S(2)}) collective-permute-start(bf16[128,1024]{1,0:T(8,128)(2,1)S(1)} %get-tuple-element.61), channel_id=1, source_target_pairs={{0,16},{32,48},{64,80},{96,112},{128,144},{160,176},{192,208},{224... | collective-permute-start | bytes 786440 | tf_op jit(solution)/shard_map/ppermute | solution.py:322
  81.9 11.3 %collective-permute-start.26 = (bf16[128,1024]{1,0:T(8,128)(2,1)S(1)}, bf16[128,1024]{1,0:T(8,128)(2,1)S(1)}, u32[]{:S(2)}, u32[]{:S(2)}) collective-permute-start(bf16[128,1024]{1,0:T(8,128)(2,1)S(1)} %get-tuple-element.73), channel_id=1, source_target_pairs={{0,16},{32,48},{64,80},{96,112},{128,144},{160,176},{192,208},{224... | collective-permute-start | bytes 786440 | tf_op jit(solution)/shard_map/ppermute | solution.py:322
  84.7 9.8 %collective-permute-start.27 = (bf16[128,1024]{1,0:T(8,128)(2,1)S(1)}, bf16[128,1024]{1,0:T(8,128)(2,1)S(1)}, u32[]{:S(2)}, u32[]{:S(2)}) collective-permute-start(bf16[128,1024]{1,0:T(8,128)(2,1)S(1)} %get-tuple-element.73), channel_id=1, source_target_pairs={{16,32},{48,64},{80,96},{112,128},{144,160},{176,192},{208,224},{2... | collective-permute-start | bytes 786440 | tf_op jit(solution)/shard_map/ppermute | solution.py:322
  87.1 7.5 %collective-permute-start.28 = (bf16[128,1024]{1,0:T(8,128)(2,1)S(1)}, bf16[128,1024]{1,0:T(8,128)(2,1)S(1)}, u32[]{:S(2)}, u32[]{:S(2)}) collective-permute-start(bf16[128,1024]{1,0:T(8,128)(2,1)S(1)} %get-tuple-element.73), channel_id=1, source_target_pairs={{0,2},{4,6},{8,10},{12,14},{2,0},{6,4},{10,8},{14,12},{1,3},{5,7},... | collective-permute-start | bytes 786440 | tf_op jit(solution)/shard_map/ppermute | solution.py:322
  87.2 11.6 %collective-permute-start.29 = (bf16[128,1024]{1,0:T(8,128)(2,1)S(1)}, bf16[128,1024]{1,0:T(8,128)(2,1)S(1)}, u32[]{:S(2)}, u32[]{:S(2)}) collective-permute-start(bf16[128,1024]{1,0:T(8,128)(2,1)S(1)} %get-tuple-element.73), channel_id=1, source_target_pairs={{2,4},{6,8},{10,12},{14,0},{4,2},{8,6},{12,10},{0,14},{3,5},{7,9},... | collective-permute-start | bytes 786440 | tf_op jit(solution)/shard_map/ppermute | solution.py:322
  93.1 8.0 %collective-permute-start.13 = (bf16[128,1024]{1,0:T(8,128)(2,1)S(1)}, bf16[128,1024]{1,0:T(8,128)(2,1)S(1)}, u32[]{:S(2)}, u32[]{:S(2)}) collective-permute-start(bf16[128,1024]{1,0:T(8,128)(2,1)S(1)} %get-tuple-element.63), channel_id=1, source_target_pairs={{0,16},{32,48},{64,80},{96,112},{128,144},{160,176},{192,208},{224... | collective-permute-start | bytes 786440 | tf_op jit(solution)/shard_map/ppermute | solution.py:322
  93.2 8.6 %collective-permute-start.14 = (bf16[128,1024]{1,0:T(8,128)(2,1)S(1)}, bf16[128,1024]{1,0:T(8,128)(2,1)S(1)}, u32[]{:S(2)}, u32[]{:S(2)}) collective-permute-start(bf16[128,1024]{1,0:T(8,128)(2,1)S(1)} %get-tuple-element.63), channel_id=1, source_target_pairs={{16,32},{48,64},{80,96},{112,128},{144,160},{176,192},{208,224},{2... | collective-permute-start | bytes 786440 | tf_op jit(solution)/shard_map/ppermute | solution.py:322
  94.6 7.3 %collective-permute-start.15 = (bf16[128,1024]{1,0:T(8,128)(2,1)S(1)}, bf16[128,1024]{1,0:T(8,128)(2,1)S(1)}, u32[]{:S(2)}, u32[]{:S(2)}) collective-permute-start(bf16[128,1024]{1,0:T(8,128)(2,1)S(1)} %get-tuple-element.63), channel_id=1, source_target_pairs={{0,2},{4,6},{8,10},{12,14},{2,0},{6,4},{10,8},{14,12},{1,3},{5,7},... | collective-permute-start | bytes 786440 | tf_op jit(solution)/shard_map/ppermute | solution.py:322
  94.6 9.5 %collective-permute-start.16 = (bf16[128,1024]{1,0:T(8,128)(2,1)S(1)}, bf16[128,1024]{1,0:T(8,128)(2,1)S(1)}, u32[]{:S(2)}, u32[]{:S(2)}) collective-permute-start(bf16[128,1024]{1,0:T(8,128)(2,1)S(1)} %get-tuple-element.63), channel_id=1, source_target_pairs={{2,4},{6,8},{10,12},{14,0},{4,2},{8,6},{12,10},{0,14},{3,5},{7,9},... | collective-permute-start | bytes 786440 | tf_op jit(solution)/shard_map/ppermute | solution.py:322
